TPU v7x, 512 devices: a whole 4x8x8 slice. The times are simulated.
512 devices in a mesh: fsdp: 128 (over y, z, core), dp: 4 (over x).
Axes of the slice: x: 4, y: 8, z: 8, core: 2. Of those that a mesh axis runs over, the one named last changes fastest.
Arguments:
- tokens: bfloat16 [512, 4096], P('dp', 'fsdp'), may hold values from -6 to 6
- out_grad: bfloat16 [512, 5120], P('dp', 'fsdp'), may hold values from -0.26367188 to 0.26367188
- master: float32 [4096, 5120], P('fsdp'), may hold values from -0.09375 to 0.09375
- moment_one: float32 [4096, 5120], P('fsdp'), may hold values from -3 to 3
- moment_two: float32 [4096, 5120], P('fsdp'), may hold values from 0.1 to 4
- flags: int32 [512, 16], P(('fsdp', 'dp')), may hold values 0 or 1
- steps: int32 [16], replicated, may hold values from 1 to 8
- rate: float32 [1], replicated, may hold values from 0.001 to 0.01
Outputs:
- master_next: float32 [4096, 5120], P('fsdp')
- moment_one_next: float32 [4096, 5120], P('fsdp')
- moment_two_next: float32 [4096, 5120], P('fsdp')
- weight_half: bfloat16 [4096, 5120], P('fsdp')
- steps_next: int32 [16], replicated
- outputs: bfloat16 [512, 5120], P('dp', 'fsdp')
All inputs are finite; a program needn't handle non-finite values. No bound on the sum of `flags` on one device may be relied on, other than what follows from the above.
Results may differ from a plain program's by a relative error of at most 0.0049.
Values may be sent and summed in bfloat16 or wider, within the bound.
No kernel may reach another device: no remote copies, remote signals or barrier semaphores. Data moves between devices by JAX's collectives and lax.ppermute only.
A program may use at most 64 MiB of HBM per device.

v0:
```python
import jax
import jax.numpy as jnp
from jax import lax
from jax.sharding import Mesh
from jax.sharding import PartitionSpec as P

BUCKETS = 16
FSDP = ("fsdp_0", "fsdp_1", "fsdp_2")
FSDP_DP = ("fsdp_0", "fsdp_1", "fsdp_2", "dp")


first_decay = 0.9
second_decay = 0.95
epsilon = 1e-08


def joined_along(blocks, dim):
    blocks = jnp.moveaxis(blocks, 0, dim)
    shape = blocks.shape
    return blocks.reshape(*shape[:dim], shape[dim] * shape[dim + 1], *shape[dim + 2 :])


def all_blocks(x, axes, order):
    blocks = x[None]
    for k in order:
        blocks = lax.all_gather(blocks, axes[k], axis=0, tiled=True)
    current = [lax.axis_size(axes[k]) for k in reversed(order)]
    blocks = blocks.reshape(*current, *x.shape)
    turned = sorted(range(len(order)), key=lambda place: order[len(order) - 1 - place])
    return blocks.transpose(*turned, *range(len(order), blocks.ndim)).reshape(-1, *x.shape)


def gather_axes(x, axes, order, dim):
    return joined_along(all_blocks(x, axes, order), dim)


def over_axes(x, axes):
    for axis in axes:
        x = lax.psum(x, axis)
    return x


def from_everyone(x, axis):
    size = lax.axis_size(axis)
    return lax.all_to_all(jnp.broadcast_to(x[None], (size, *x.shape)), axis, 0, 0, tiled=True)


def of_everyone(x, axis):
    everything = from_everyone(x, axis)
    return jnp.sum(everything, axis=0)


def local(tokens, out_grad, master, moment_one, moment_two, flags, steps, rate):
    width_out = master.shape[1]
    bucket_width = width_out // BUCKETS
    contract_rows = (((0,), (0,)), ((), ()))
    partial_value = lax.dot_general(
        tokens,
        gather_axes(out_grad, (("fsdp_0", "fsdp_1"), "fsdp_2"), (0, 1), 1),
        contract_rows,
        preferred_element_type=jnp.float32,
    )
    counts = over_axes(flags[0], FSDP_DP)
    gradient = of_everyone(partial_value, "dp")
    commit_bucket = counts == 0
    commit = jnp.repeat(commit_bucket, bucket_width)[None, :]
    times = jnp.repeat(steps + 1, bucket_width).astype(jnp.float32)[None, :]
    first = first_decay * moment_one + (1.0 - first_decay) * gradient
    second = second_decay * moment_two + (1.0 - second_decay) * gradient * gradient
    fix_one = 1.0 - jnp.power(jnp.float32(first_decay), times)
    fix_two = 1.0 - jnp.power(jnp.float32(second_decay), times)
    candidate = master - rate[0] * (first / fix_one) / (jnp.sqrt(second / fix_two) + epsilon)
    master_next = jnp.where(commit, candidate, master)
    moment_one_next = jnp.where(commit, first, moment_one)
    moment_two_next = jnp.where(commit, second, moment_two)
    weight_half = master_next.astype(jnp.bfloat16)
    steps_next = steps + commit_bucket.astype(jnp.int32)
    weight_cols = lax.all_to_all(weight_half, FSDP, split_axis=1, concat_axis=0, tiled=True)
    result = jnp.dot(
        lax.all_gather(tokens, FSDP, axis=1, tiled=True),
        weight_cols,
        preferred_element_type=jnp.float32,
    )
    return (
        master_next,
        moment_one_next,
        moment_two_next,
        weight_half,
        steps_next,
        result.astype(jnp.bfloat16),
    )


def solution(mesh):
    split = Mesh(
        mesh.devices.reshape(8, 8, 2, mesh.shape["dp"]), ("fsdp_0", "fsdp_1", "fsdp_2", "dp")
    )
    in_specs = (
        P("dp", FSDP),
        P("dp", FSDP),
        P(FSDP, None),
        P(FSDP, None),
        P(FSDP, None),
        P(FSDP_DP, None),
        P(),
        P(),
    )
    out_specs = (P(FSDP, None), P(FSDP, None), P(FSDP, None), P(FSDP, None), P(), P("dp", FSDP))
    return jax.shard_map(local, mesh=split, in_specs=in_specs, out_specs=out_specs, check_vma=False)
```

profile of v0, /device:TPU:1, one launch (start us, length us, event | category | flops | bytes accessed | tf_op | source)
XLA Modules:
  0.0 188.4 jit_solution(5304647750274123168)
XLA Ops:
  8.0 47.0 %all-gather = bf16[8192,40]{0,1:T(8,128)(2,1)S(1)} all-gather(bf16[128,40]{0,1:T(8,128)(2,1)} %param.9), channel_id=2, replica_groups=mesh['fsdp_0'=8,'fsdp_1'=8,'fsdp_2'=2,'dp'=4] {'fsdp_0','fsdp_1'}, dimensions={0}, use_global_device_ids=true | all-gather | bytes 665600 | tf_op jit(solution)/shard_map/all_gather | solution.py:26
  55.1 1.0 copy.30
  56.1 26.5 %all-gather.4.cloned.1.call-done = bf16[128,128,40]{1,0,2:T(8,128)(2,1)} async-done(((bf16[64,128,40]{1,0,2:T(8,128)(2,1)}), bf16[128,128,40]{1,0,2:T(8,128)(2,1)}) %all-gather.4.cloned.1.call-update) | async-done | bytes 1310736 | tf_op jit(solution)/shard_map/all_gather | solution.py:26
  82.6 2.2 %copy.25 = bf16[64,2,128,40]{2,3,1,0:T(8,128)(2,1)S(1)} copy(bf16[64,2,128,40]{2,0,1,3:T(8,128)(2,1)} %bitcast.33) | data formatting | bytes 2621440 | tf_op jit(solution)/shard_map/transpose | solution.py:30
  84.8 0.5 fusion.5
  85.3 1.8 broadcast_in_dim.38
  87.1 3.8 %all-to-all-start = ((f32[4,32,5120]{2,1,0:T(8,128)}), f32[4,32,5120]{2,1,0:T(8,128)S(1)}, u32[]{:S(2)}, u32[]{:S(2)}) async-start(f32[4,32,5120]{2,1,0:T(8,128)} %broadcast_in_dim.38), calls=%async_computation | async-start | bytes 5242880 | tf_op jit(solution)/shard_map/all_to_all | solution.py:45
  91.0 0.5 all-gather.6.cloned.1.call-update
  92.5 10.5 %psum.28 = s32[16]{0:T(128)S(1)} all-reduce(s32[16]{0:T(128)S(1)} %bitcast.34), channel_id=1, replica_groups=mesh['fsdp_0'=8,'fsdp_1'=8,'fsdp_2'=2,'dp'=4] {'fsdp_0'}, use_global_device_ids=true, to_apply=%region_0.0 | all-reduce | flops 16 | bytes 128 | tf_op jit(solution)/shard_map/psum | solution.py:39
  103.0 12.2 %psum.29 = s32[16]{0:T(128)S(1)} all-reduce(s32[16]{0:T(128)S(1)} %psum.28), channel_id=1, replica_groups=mesh['fsdp_0'=8,'fsdp_1'=8,'fsdp_2'=2,'dp'=4] {'fsdp_1'}, use_global_device_ids=true, to_apply=%region_1.0 | all-reduce | flops 16 | bytes 128 | tf_op jit(solution)/shard_map/psum | solution.py:39
  115.2 6.6 %psum.30 = s32[16]{0:T(128)S(1)} all-reduce(s32[16]{0:T(128)S(1)} %psum.29), channel_id=1, replica_groups=mesh['fsdp_0'=8,'fsdp_1'=8,'fsdp_2'=2,'dp'=4] {'fsdp_2'}, use_global_device_ids=true, to_apply=%region_2.0 | all-reduce | flops 16 | bytes 128 | tf_op jit(solution)/shard_map/psum | solution.py:39
  121.8 7.3 %psum.31 = s32[16]{0:T(128)S(1)} all-reduce(s32[16]{0:T(128)S(1)} %psum.30), channel_id=1, replica_groups=mesh['fsdp_0'=8,'fsdp_1'=8,'fsdp_2'=2,'dp'=4] {'dp'}, use_global_device_ids=true, to_apply=%region_3.0 | all-reduce | flops 16 | bytes 128 | tf_op jit(solution)/shard_map/psum | solution.py:39
  129.2 0.1 broadcast_in_dim.35
  129.3 0.2 reduce_sum.9
  129.5 3.1 %fusion.4 = (bf16[32,5120]{1,0:T(8,128)(2,1)S(1)}, f32[32,5120]{1,0:T(8,128)}, f32[32,5120]{1,0:T(8,128)}, f32[32,5120]{1,0:T(8,128)}) fusion(f32[32,5120]{1,0:T(8,128)} %param.10, f32[5120]{0:T(1024)S(1)} %sub.30, f32[32,5120]{1,0:T(8,128)S(1)} %reduce_sum.9, f32[32,5120]{1,0:T(8,128)} %param.12, f32[5120]{0:T(1024)S(1)} %sub.28, f32[32,5120]{1,0:T(8,128)} %param.11, ...), kind=kLoop, calls=%fused_computation.12 | loop fusion | flops 2785280 | bytes 4961284 | tf_op jit(solution)/shard_map/convert_element_type | solution.py:76
  132.6 1.9 all_to_all.18
  134.5 0.7 copy.32
  135.2 2.4 %reshape.56 = bf16[128,2,640]{2,1,0:T(2,128)(2,1)} reshape(bf16[128,32,40]{2,1,0:T(8,128)(2,1)S(1)} %bitcast.30) | data formatting | bytes 655360
  137.6 10.5 %all-to-all-start.1 = ((bf16[128,2,640]{2,1,0:T(2,128)(2,1)}), bf16[128,2,640]{2,1,0:T(2,128)(2,1)S(1)}, u32[]{:S(2)}, u32[]{:S(2)}) async-start(bf16[128,2,640]{2,1,0:T(2,128)(2,1)} %reshape.56), calls=%async_computation.1 | async-start | bytes 655360 | tf_op jit(solution)/shard_map/all_to_all | solution.py:78
  148.0 0.5 convert_add_fusion
  148.6 15.3 %all-to-all-done.1 = bf16[128,2,640]{2,1,0:T(2,128)(2,1)S(1)} async-done(((bf16[128,2,640]{2,1,0:T(2,128)(2,1)}), bf16[128,2,640]{2,1,0:T(2,128)(2,1)S(1)}, u32[]{:S(2)}, u32[]{:S(2)}) %all-to-all-start.1) | async-done | bytes 327712 | tf_op jit(solution)/shard_map/all_to_all | solution.py:78
  163.9 1.6 reshape.57
  165.5 13.2 %all-gather.6.cloned.1.call-done = bf16[128,4096]{0,1:T(8,128)(2,1)} async-done(((bf16[128,32]{0,1:T(8,128)(2,1)}), bf16[128,4096]{0,1:T(8,128)(2,1)}) %all-gather.6.cloned.1.call-update) | async-done | bytes 1048592 | tf_op jit(solution)/shard_map/all_gather | solution.py:80
  178.7 2.3 %fusion = bf16[128,40]{0,1:T(8,128)(2,1)} fusion(bf16[4096,40]{1,0:T(8,128)(2,1)S(1)} %bitcast.29, bf16[128,4096]{0,1:T(8,128)(2,1)} %all-gather.6.cloned.1.call-done), kind=kOutput, calls=%fused_computation.1 | convolution fusion | flops 41948160 | bytes 1386496 | tf_op jit(solution)/shard_map/dot_general | solution.py:79
  (19 shorter events, 0.5 us)
Async XLA Ops:
  8.0 74.6 %all-gather.4.cloned.1.call-start = ((), (), s32[]{:S(2)}) async-start(), calls=%async_computation.2 | async-start | bytes 1966080 | tf_op jit(solution)/shard_map/all_gather | solution.py:26
  82.6 2.2 %copy-start.1 = (bf16[128,32]{0,1:T(8,128)(2,1)S(1)}, bf16[128,32]{0,1:T(8,128)(2,1)}, u32[]{:S(2)}) copy-start(bf16[128,32]{0,1:T(8,128)(2,1)} %param.8) | copy-start | bytes 24580
  87.1 4.4 %copy-start.3 = (s32[16]{0:T(128)S(1)}, s32[16]{0:T(128)}, u32[]{:S(2)}) copy-start(s32[16]{0:T(128)} %param.14) | copy-start | bytes 196
  87.1 5.4 %copy-start.2 = (s32[1,16]{1,0:T(1,128)S(1)}, s32[1,16]{1,0:T(1,128)}, u32[]{:S(2)}) copy-start(s32[1,16]{1,0:T(1,128)} %param.13) | copy-start | bytes 196
  87.1 42.2 %all-to-all-start = ((f32[4,32,5120]{2,1,0:T(8,128)}), f32[4,32,5120]{2,1,0:T(8,128)S(1)}, u32[]{:S(2)}, u32[]{:S(2)}) async-start(f32[4,32,5120]{2,1,0:T(8,128)} %broadcast_in_dim.38), calls=%async_computation | async-start | bytes 5242880 | tf_op jit(solution)/shard_map/all_to_all | solution.py:45
  90.9 87.8 %all-gather.6.cloned.1.call-start = ((), (), s32[]{:S(2)}) async-start(), calls=%async_computation.3 | async-start | bytes 1056768 | tf_op jit(solution)/shard_map/all_gather | solution.py:80
  132.6 2.6 %copy-start = (bf16[32,5120]{1,0:T(8,128)(2,1)}, bf16[32,5120]{1,0:T(8,128)(2,1)S(1)}, u32[]{:S(2)}) copy-start(bf16[32,5120]{1,0:T(8,128)(2,1)S(1)} %get-tuple-element.6) | copy-start | bytes 983044
  137.6 26.3 %all-to-all-start.1 = ((bf16[128,2,640]{2,1,0:T(2,128)(2,1)}), bf16[128,2,640]{2,1,0:T(2,128)(2,1)S(1)}, u32[]{:S(2)}, u32[]{:S(2)}) async-start(bf16[128,2,640]{2,1,0:T(2,128)(2,1)} %reshape.56), calls=%async_computation.1 | async-start | bytes 655360 | tf_op jit(solution)/shard_map/all_to_all | solution.py:78
Sparse Core Ops, SparseCore 0:
  56.2 26.3 all-gather.3
Sparse Core Ops, SparseCore 1:
  94.4 84.3 all-gather.5
where the time goes:
time: 189 us; the launch traced here: 188 us
  blocking collectives  83.7 us (44%)
  waiting for transfers between devices  55.6 us (29%)
  between operations  16.2 us (9%)
  starting transfers between devices  14.3 us (8%)
  local copies, waits for them, and re-layouts  12 us (6%)
  other arithmetic  3.83 us (2%)
  matrix products  2.8 us (1%)
    all_gather x1, blocking collectives, all_blocks(): blocks = lax.all_gather(blocks, axes[k], axis=0, tiled=True)  47 us
    psum x4, blocking collectives, over_axes(): x = lax.psum(x, axis)  36.6 us
    all_gather x1, waiting for transfers between devices, all_blocks(): blocks = lax.all_gather(blocks, axes[k], axis=0, tiled=True)  26.5 us
    all_to_all x1, waiting for transfers between devices, local(): lax.all_to_all(weight_half, FSDP, split_axis=1, concat_axis=0, tiled=True)  15.3 us
    all_gather x1, waiting for transfers between devices, local(): lax.all_gather(tokens, FSDP, axis=1, tiled=True)  13.2 us
    all_to_all x1, starting transfers between devices, local(): lax.all_to_all(weight_half, FSDP, split_axis=1, concat_axis=0, tiled=True)  10.5 us
    unnamed x11, local copies, waits for them, and re-layouts  4.98 us
    all_to_all x1, starting transfers between devices, from_everyone(): lax.all_to_all(jnp.broadcast_to(x[None], (size, *x.shape)), axis, 0, 0, t...  3.78 us
  transfers between devices with their start and end apart: 4, of which 3 were waited for; matrix products, arithmetic and copies ran while one was open for 5% of the time, Pallas kernels for 0%

commit v1 on v0

v1 whole, which is shorter than its diff:
```python
import jax
import jax.numpy as jnp
from jax import lax
from jax.sharding import Mesh
from jax.sharding import PartitionSpec as P

BUCKETS = 16
FSDP = ("y", "zh", "zl", "c")
ALL = FSDP + ("x",)
ZC = ("zh", "zl", "c")
XY = ("x", "y")
NX, NY, NZC = 4, 8, 16
first_decay = 0.9
second_decay = 0.95
epsilon = 1e-08
bf16, f32 = jnp.bfloat16, jnp.float32


def exchange(x, axes):
    return lax.all_to_all(x, axes, 0, 0, tiled=True)


def everyone(x, axes, n):
    return exchange(jnp.broadcast_to(x[None], (n, *x.shape)), axes)


def adam(master, one, two, gradient, commit, times, rate):
    first = first_decay * one + (1.0 - first_decay) * gradient
    second = second_decay * two + (1.0 - second_decay) * gradient * gradient
    fix_one = 1.0 - jnp.power(f32(first_decay), times)
    fix_two = 1.0 - jnp.power(f32(second_decay), times)
    candidate = master - rate * (first / fix_one) / (jnp.sqrt(second / fix_two) + epsilon)
    return (
        jnp.where(commit, candidate, master),
        jnp.where(commit, first, one),
        jnp.where(commit, second, two),
    )


def local(tokens, out_grad, master, moment_one, moment_two, flags, steps, rate):
    rows, width = master.shape
    bucket_width = width // BUCKETS
    tok_g, chunk = out_grad.shape
    cols = chunk * NZC // NX
    ix, iy = lax.axis_index("x"), lax.axis_index("y")
    lanes = 128

    mine = jnp.pad(flags.astype(bf16), ((0, 7), (0, lanes - BUCKETS)))
    seen = jnp.max(everyone(mine, XY, NX * NY), axis=0)

    tok = everyone(tokens.T, XY, NX * NY).reshape(NX, NY * rows, tok_g)

    perm = [(zh * NX + x, x * NX + zh) for zh in range(NX) for x in range(NX)]
    og = lax.ppermute(out_grad.T, ("zh", "x"), perm)
    og = everyone(jnp.concatenate([og, seen], axis=0), ZC, NZC)
    counts = jnp.max(og[:, chunk, :BUCKETS], axis=0)
    og = og[:, :chunk].reshape(NX, cols, tok_g)
    commit_bucket = counts == 0

    def block(p):
        q = lax.dynamic_index_in_dim(p.reshape(rows, NY, NX, cols), ix, 2, keepdims=False)
        return q.transpose(1, 0, 2)

    high = master.astype(bf16)
    low = (master - high.astype(f32)).astype(bf16)
    params = jnp.concatenate(
        [block(high), block(low), block(moment_one.astype(bf16)), block(moment_two.astype(bf16))], axis=2
    )
    params = exchange(params, "y").reshape(NY * rows, 4 * cols).astype(f32)
    b_master = params[:, :cols] + params[:, cols : 2 * cols]
    b_one = params[:, 2 * cols : 3 * cols]
    b_two = params[:, 3 * cols :]

    grad = sum(
        lax.dot_general(tok[k], og[k], (((1,), (1,)), ((), ())), preferred_element_type=f32) for k in range(NX)
    )
    send = jnp.broadcast_to(grad.astype(bf16).reshape(1, NY, rows, cols), (NX, NY, rows, cols))
    full = exchange(send.reshape(NX * NY, rows, cols), XY)
    full = full.reshape(NX, NY, rows, cols).transpose(2, 1, 0, 3).reshape(rows, width).astype(f32)

    bucket = (iy * NX + ix) * cols // bucket_width
    b_times = (steps[bucket] + 1).astype(f32)
    half, _, _ = adam(b_master, b_one, b_two, grad, commit_bucket[bucket], b_times, rate[0])
    half = half.astype(bf16)
    part = lax.dot_general(
        tok, half, (((1,), (0,)), ((), ())), preferred_element_type=f32
    )
    part = part.transpose(0, 2, 1).reshape(NZC, chunk, tok_g)
    total = jnp.sum(exchange(part, ZC), axis=0)
    result = lax.ppermute(total.astype(bf16), ("zh", "x"), perm).T

    commit = jnp.repeat(commit_bucket, bucket_width)[None, :]
    times = jnp.repeat(steps + 1, bucket_width).astype(f32)[None, :]
    master_next, one_next, two_next = adam(master, moment_one, moment_two, full, commit, times, rate[0])
    steps_next = steps + commit_bucket.astype(jnp.int32)
    return master_next, one_next, two_next, master_next.astype(bf16), steps_next, result


def solution(mesh):
    split = Mesh(mesh.devices.reshape(8, 4, 2, 2, 4), ALL)
    in_specs = (P("x", FSDP), P("x", FSDP), P(FSDP), P(FSDP), P(FSDP), P(ALL), P(), P())
    out_specs = (P(FSDP), P(FSDP), P(FSDP), P(FSDP), P(), P("x", FSDP))
    return jax.shard_map(local, mesh=split, in_specs=in_specs, out_specs=out_specs, check_vma=False)
```

time: 189 us -> 145 us (0.77)
  the two profiles are of different devices: /device:TPU:1 before, /device:TPU:5 now
where the time goes in v1:
time: 145 us
  starting transfers between devices  48.3 us (33%)
  waiting for transfers between devices  38.6 us (27%)
  blocking collectives  36.7 us (25%)
  local copies, waits for them, and re-layouts  10.9 us (8%)
  other arithmetic  6.15 us (4%)
  between operations  2.31 us (2%)
  matrix products  1.59 us (1%)
    all_to_all x2, blocking collectives, exchange(): return lax.all_to_all(x, axes, 0, 0, tiled=True)  36.7 us
    all_to_all x4, starting transfers between devices, exchange(): return lax.all_to_all(x, axes, 0, 0, tiled=True)  34.3 us
    all_to_all x4, waiting for transfers between devices, exchange(): return lax.all_to_all(x, axes, 0, 0, tiled=True)  30.8 us
    ppermute x1, starting transfers between devices, local(): og = lax.ppermute(out_grad.T, ('zh', 'x'), perm)  10.6 us
    ppermute x1, waiting for transfers between devices, local(): result = lax.ppermute(total.astype(bf16), ('zh', 'x'), perm).T  6.74 us
    convert_element_type x1, other arithmetic, local(): master_next.astype(bf16)  3.72 us
    ppermute x1, starting transfers between devices, local(): result = lax.ppermute(total.astype(bf16), ('zh', 'x'), perm).T  3.46 us
  transfers between devices with their start and end apart: 6, of which 5 were waited for; matrix products, arithmetic and copies ran while one was open for 2% of the time, Pallas kernels for 0%

profile of v1, /device:TPU:5, one launch (start us, length us, event | category | flops | bytes accessed | tf_op | source)
XLA Modules:
  0.0 144.6 jit_solution(16539667208473164660)
XLA Ops:
  0.6 0.7 convert_element_type.69
  1.3 0.6 broadcast_in_dim.50
  1.9 9.8 %all-to-all-start = ((bf16[32,8,128]{2,1,0:T(8,128)(2,1)}), bf16[32,8,128]{2,1,0:T(8,128)(2,1)S(1)}, u32[]{:S(2)}, u32[]{:S(2)}) async-start(bf16[32,8,128]{2,1,0:T(8,128)(2,1)} %broadcast_in_dim.50), calls=%async_computation | async-start | bytes 131072 | tf_op jit(solution)/shard_map/all_to_all | solution.py:20
  11.8 10.6 %collective-permute-start = (bf16[40,128]{1,0:T(8,128)(2,1)S(1)}, bf16[40,128]{1,0:T(8,128)(2,1)S(1)}, u32[]{:S(2)}, u32[]{:S(2)}) collective-permute-start(bf16[40,128]{1,0:T(8,128)(2,1)S(1)} %bitcast.82), channel_id=1, source_target_pairs={{0,0},{1,16},{2,32},{3,48},{16,1},{17,17},{18,33},{19,49},{32,2},{... | collective-permute-start | bytes 30728 | tf_op jit(solution)/shard_map/ppermute | solution.py:54
  22.4 1.0 collective-permute-done
  23.5 18.0 %all_to_all.30 = bf16[16,48,128]{2,1,0:T(8,128)(2,1)S(1)} all-to-all(bf16[16,48,128]{2,1,0:T(8,128)(2,1)S(1)} %broadcast_in_dim.51), channel_id=1, replica_groups=mesh['y'=8,'zh'=4,'zl'=2,'c'=2,'x'=4] {'zh','zl','c'}, dimensions={0} | all-to-all | bytes 393216 | tf_op jit(solution)/shard_map/all_to_all | solution.py:20
  41.5 0.7 broadcast_in_dim.55
  42.2 11.5 %all-to-all-start.2 = ((bf16[32,32,128]{2,1,0:T(8,128)(2,1)}), bf16[32,32,128]{2,1,0:T(8,128)(2,1)S(1)}, u32[]{:S(2)}, u32[]{:S(2)}) async-start(bf16[32,32,128]{2,1,0:T(8,128)(2,1)} %broadcast_in_dim.55), calls=%async_computation.2 | async-start | bytes 524288 | tf_op jit(solution)/shard_map/all_to_all | solution.py:20
  53.7 9.5 %all-to-all-done.2 = bf16[32,32,128]{2,1,0:T(8,128)(2,1)S(1)} async-done(((bf16[32,32,128]{2,1,0:T(8,128)(2,1)}), bf16[32,32,128]{2,1,0:T(8,128)(2,1)S(1)}, u32[]{:S(2)}, u32[]{:S(2)}) %all-to-all-start.2) | async-done | bytes 262176 | tf_op jit(solution)/shard_map/all_to_all | solution.py:20
  64.1 0.9 broadcast_in_dim.57
  65.0 7.3 %all-to-all-start.3 = ((bf16[32,32,160]{2,1,0:T(8,128)(2,1)}), bf16[32,32,160]{2,1,0:T(8,128)(2,1)S(1)}, u32[]{:S(2)}, u32[]{:S(2)}) async-start(bf16[32,32,160]{2,1,0:T(8,128)(2,1)} %bitcast.13), calls=%async_computation.3 | async-start | bytes 1048576 | tf_op jit(solution)/shard_map/all_to_all | solution.py:20
  73.5 12.0 %all-to-all-done.3 = bf16[32,32,160]{2,1,0:T(8,128)(2,1)S(1)} async-done(((bf16[32,32,160]{2,1,0:T(8,128)(2,1)}), bf16[32,32,160]{2,1,0:T(8,128)(2,1)S(1)}, u32[]{:S(2)}, u32[]{:S(2)}) %all-to-all-start.3) | async-done | bytes 327712 | tf_op jit(solution)/shard_map/all_to_all | solution.py:20
  85.6 0.7 copy.50
  86.3 1.0 reshape.109
  87.4 3.7 %fusion.18 = (bf16[32,5120]{1,0:T(8,128)(2,1)}, f32[32,5120]{1,0:T(8,128)}, f32[32,5120]{1,0:T(8,128)}, f32[32,5120]{1,0:T(8,128)}, bf16[32,5120]{1,0:T(8,128)(2...) fusion(f32[32,5120]{1,0:T(8,128)S(1)} %copy-done, ...), kind=kLoop, calls=%fused_computation.43 | loop fusion | flops 3768320 | bytes 6272004 | tf_op jit(solution)/shard_map/convert_element_type | solution.py:96
  95.0 0.9 pad_maximum_fusion
  95.9 5.7 %all-to-all-start.4 = ((bf16[8,32,640]{2,1,0:T(8,128)(2,1)}), bf16[8,32,640]{2,1,0:T(8,128)(2,1)S(1)}, u32[]{:S(2)}, u32[]{:S(2)}) async-start(bf16[8,32,640]{2,1,0:T(8,128)(2,1)} %pad_maximum_fusion), calls=%async_computation.4 | async-start | bytes 655360 | tf_op jit(solution)/shard_map/all_to_all | solution.py:20
  102.9 0.6 dynamic_slice.19
  103.6 9.3 %all-to-all-done.4 = bf16[8,32,640]{2,1,0:T(8,128)(2,1)S(1)} async-done(((bf16[8,32,640]{2,1,0:T(8,128)(2,1)}), bf16[8,32,640]{2,1,0:T(8,128)(2,1)S(1)}, u32[]{:S(2)}, u32[]{:S(2)}) %all-to-all-start.4) | async-done | bytes 327712 | tf_op jit(solution)/shard_map/all_to_all | solution.py:20
  113.6 0.9 fusion.10
  114.5 18.7 %all_to_all.31 = f32[16,40,128]{2,1,0:T(8,128)S(1)} all-to-all(f32[16,40,128]{2,1,0:T(8,128)S(1)} %bitcast.71), channel_id=1, replica_groups=mesh['y'=8,'zh'=4,'zl'=2,'c'=2,'x'=4] {'zh','zl','c'}, dimensions={0} | all-to-all | bytes 655360 | tf_op jit(solution)/shard_map/all_to_all | solution.py:20
  133.2 3.5 %collective-permute-start.1 = (bf16[40,128]{1,0:T(8,128)(2,1)S(1)}, bf16[40,128]{1,0:T(8,128)(2,1)S(1)}, u32[]{:S(2)}, u32[]{:S(2)}) collective-permute-start(bf16[40,128]{1,0:T(8,128)(2,1)S(1)} %reduce_sum.9), channel_id=1, source_target_pairs={{0,0},{1,16},{2,32},{3,48},{16,1},{17,17},{18,33},{19,49},{32,2},{... | collective-permute-start | bytes 30728 | tf_op jit(solution)/shard_map/ppermute | solution.py:90
  137.2 6.7 %collective-permute-done.1 = bf16[40,128]{1,0:T(8,128)(2,1)S(1)} collective-permute-done((bf16[40,128]{1,0:T(8,128)(2,1)S(1)}, bf16[40,128]{1,0:T(8,128)(2,1)S(1)}, u32[]{:S(2)}, u32[]{:S(2)}) %collective-permute-start.1) | collective-permute-done | bytes 10272 | tf_op jit(solution)/shard_map/ppermute | solution.py:90
  144.0 0.6 copy.78
  (49 shorter events, 7.3 us)
Async XLA Ops:
  1.9 9.8 %copy-start.2 = (bf16[128,40]{0,1:T(8,128)(2,1)S(1)}, bf16[128,40]{0,1:T(8,128)(2,1)}, u32[]{:S(2)}) copy-start(bf16[128,40]{0,1:T(8,128)(2,1)} %param.9) | copy-start | bytes 30724
  1.9 20.4 %all-to-all-start = ((bf16[32,8,128]{2,1,0:T(8,128)(2,1)}), bf16[32,8,128]{2,1,0:T(8,128)(2,1)S(1)}, u32[]{:S(2)}, u32[]{:S(2)}) async-start(bf16[32,8,128]{2,1,0:T(8,128)(2,1)} %broadcast_in_dim.50), calls=%async_computation | async-start | bytes 131072 | tf_op jit(solution)/shard_map/all_to_all | solution.py:20
  11.8 11.6 %collective-permute-start = (bf16[40,128]{1,0:T(8,128)(2,1)S(1)}, bf16[40,128]{1,0:T(8,128)(2,1)S(1)}, u32[]{:S(2)}, u32[]{:S(2)}) collective-permute-start(bf16[40,128]{1,0:T(8,128)(2,1)S(1)} %bitcast.82), channel_id=1, source_target_pairs={{0,0},{1,16},{2,32},{3,48},{16,1},{17,17},{18,33},{19,49},{32,2},{... | collective-permute-start | bytes 30728 | tf_op jit(solution)/shard_map/ppermute | solution.py:54
  23.4 18.0 %copy-start.1 = (bf16[128,32]{0,1:T(8,128)(2,1)S(1)}, bf16[128,32]{0,1:T(8,128)(2,1)}, u32[]{:S(2)}) copy-start(bf16[128,32]{0,1:T(8,128)(2,1)} %param.8) | copy-start | bytes 24580
  42.2 21.1 %all-to-all-start.2 = ((bf16[32,32,128]{2,1,0:T(8,128)(2,1)}), bf16[32,32,128]{2,1,0:T(8,128)(2,1)S(1)}, u32[]{:S(2)}, u32[]{:S(2)}) async-start(bf16[32,32,128]{2,1,0:T(8,128)(2,1)} %broadcast_in_dim.55), calls=%async_computation.2 | async-start | bytes 524288 | tf_op jit(solution)/shard_map/all_to_all | solution.py:20
  65.0 20.6 %all-to-all-start.3 = ((bf16[32,32,160]{2,1,0:T(8,128)(2,1)}), bf16[32,32,160]{2,1,0:T(8,128)(2,1)S(1)}, u32[]{:S(2)}, u32[]{:S(2)}) async-start(bf16[32,32,160]{2,1,0:T(8,128)(2,1)} %bitcast.13), calls=%async_computation.3 | async-start | bytes 1048576 | tf_op jit(solution)/shard_map/all_to_all | solution.py:20
  72.3 0.7 copy-start.3
  86.3 1.1 copy-start
  95.9 16.9 %all-to-all-start.4 = ((bf16[8,32,640]{2,1,0:T(8,128)(2,1)}), bf16[8,32,640]{2,1,0:T(8,128)(2,1)S(1)}, u32[]{:S(2)}, u32[]{:S(2)}) async-start(bf16[8,32,640]{2,1,0:T(8,128)(2,1)} %pad_maximum_fusion), calls=%async_computation.4 | async-start | bytes 655360 | tf_op jit(solution)/shard_map/all_to_all | solution.py:20
  133.2 10.7 %collective-permute-start.1 = (bf16[40,128]{1,0:T(8,128)(2,1)S(1)}, bf16[40,128]{1,0:T(8,128)(2,1)S(1)}, u32[]{:S(2)}, u32[]{:S(2)}) collective-permute-start(bf16[40,128]{1,0:T(8,128)(2,1)S(1)} %reduce_sum.9), channel_id=1, source_target_pairs={{0,0},{1,16},{2,32},{3,48},{16,1},{17,17},{18,33},{19,49},{32,2},{... | collective-permute-start | bytes 30728 | tf_op jit(solution)/shard_map/ppermute | solution.py:90

commit v2 on v1

v2 whole, which is shorter than its diff:
```python
import jax
import jax.numpy as jnp
from jax import lax
from jax.experimental import pallas as pl
from jax.experimental.pallas import tpu as pltpu
from jax.sharding import Mesh
from jax.sharding import PartitionSpec as P

BUCKETS = 16
FSDP = ("y", "zh", "zl", "c")
ALL = FSDP + ("x",)
ZC = ("zh", "zl", "c")
XY = ("x", "y")
NX, NY, NZC = 4, 8, 16
LANES = 128
first_decay = 0.9
second_decay = 0.95
epsilon = 1e-08
bf16, f32 = jnp.bfloat16, jnp.float32
VMEM, SMEM = pltpu.VMEM, pltpu.SMEM
SMALL = pltpu.CompilerParams(vmem_limit_bytes=16 * 1024 * 1024)


def exchange(x, axes):
    return lax.all_to_all(x, axes, 0, 0, tiled=True)


def pack_kernel(ix_ref, tok_ref, flag_ref, master_ref, one_ref, two_ref, out_ref):
    tok = tok_ref[...]
    flag = flag_ref[...]
    master = master_ref[...]
    high = master.astype(bf16).astype(f32)
    parts = (high, master - high, one_ref[...], two_ref[...])
    for x in range(NX):
        for y in range(NY):
            c = (y * NX + x) * 160
            d = x * NY + y
            out_ref[d, 0:32, :] = tok
            main = [p[:, c : c + LANES] for p in parts]
            rest = jnp.concatenate([p[:, c + LANES : c + 160] for p in parts], axis=1)
            out_ref[d, 32:48, :] = jnp.concatenate(main[:2], axis=0).astype(bf16)
            out_ref[d, 48:64, :] = jnp.concatenate(main[2:], axis=0).astype(bf16)
            out_ref[d, 64:80, :] = jnp.concatenate([rest, flag], axis=0).astype(bf16)


def pack(ix, tok, flag, master, one, two):
    rows = master.shape[0] // NX
    part = pl.BlockSpec((rows, master.shape[1]), lambda i, ix: (ix[0], 0))
    whole = lambda a: pl.BlockSpec(a.shape, lambda i, ix: (0, 0))
    return pl.pallas_call(
        pack_kernel,
        out_shape=jax.ShapeDtypeStruct((NX * NY, 80, LANES), bf16),
        grid_spec=pltpu.PrefetchScalarGridSpec(
            num_scalar_prefetch=1,
            grid=(1,),
            in_specs=[whole(tok), whole(flag), part, part, part],
            out_specs=pl.BlockSpec((NX * NY, 80, LANES), lambda i, ix: (0, 0, 0)),
        ),
        name="pack",
    )(ix, tok, flag, master, one, two)


def update(master, one, two, gradient, scale, fix):
    first = first_decay * one + (1.0 - first_decay) * gradient
    second = second_decay * two + (1.0 - second_decay) * gradient * gradient
    return master - scale * first / (jnp.sqrt(second * fix) + epsilon), first, second


def block_kernel(bucket_ref, scale_ref, fix_ref, first_ref, second_ref, grad_ref, part_ref, count_ref, params):
    tok = [first_ref[x * NY : (x + 1) * NY, 0:32, :].reshape(NY * 32, LANES) for x in range(NX)]
    og = [second_ref[x * NX : (x + 1) * NX, 0:40, :].reshape(160, LANES) for x in range(NX)]
    grad = jnp.zeros((NY * 32, 160), f32)
    for x in range(NX):
        grad += lax.dot_general(tok[x], og[x], (((1,), (1,)), ((), ())), preferred_element_type=f32)
    for y in range(NY):
        g = grad[y * 32 : (y + 1) * 32, :]
        tail = jnp.concatenate([g[8 * k : 8 * k + 8, LANES:160] for k in range(4)], axis=1)
        g = jnp.concatenate([g[:, :LANES], tail], axis=0).astype(bf16)
        for x in range(NX):
            grad_ref[x * NY + y] = g
    count = jnp.max(second_ref[:, 40:48, :].astype(f32), axis=0)
    count_ref[...] = count
    lane = lax.broadcasted_iota(jnp.int32, (8, LANES), 1)
    mine = jnp.max(jnp.where(lane == bucket_ref[0], count, 0.0), axis=(0, 1), keepdims=True)
    for x in range(NX):
        for y in range(NY):
            r = y * 32 + x * 8
            for k in range(2):
                two = first_ref[x * NY + y, 32 + 16 * k : 48 + 16 * k, :].astype(f32)
                params[2 * k, r : r + 8, :] = two[:8]
                params[2 * k + 1, r : r + 8, :] = two[8:]
            params[4, r : r + 8, :] = first_ref[x * NY + y, 64:80, :].astype(f32)[:8]
    scale, fix = scale_ref[bucket_ref[0]], fix_ref[bucket_ref[0]]
    halves = []
    for lo, hi in ((0, LANES), (LANES, 160)):
        if lo == 0:
            p = [params[k] for k in range(4)]
        else:
            rest = params[4]
            p = [rest[:, 32 * k : 32 * k + 32] for k in range(4)]
        old = p[0] + p[1]
        new, _, _ = update(old, p[2], p[3], grad[:, lo:hi], scale, fix)
        halves.append(jnp.where(mine == 0.0, new, old))
    weight = jnp.concatenate(halves, axis=1).T.astype(bf16)
    for x in range(NX):
        out = jnp.dot(weight, tok[x], preferred_element_type=f32)
        for k in range(NX):
            part_ref[x * NX + k] = out[40 * k : 40 * k + 40, :]


def block(bucket, scale, fix, first, second):
    smem, vmem = pl.BlockSpec(memory_space=SMEM), pl.BlockSpec(memory_space=VMEM)
    return pl.pallas_call(
        block_kernel,
        out_shape=(
            jax.ShapeDtypeStruct((NX * NY, 40, LANES), bf16),
            jax.ShapeDtypeStruct((NZC, 40, LANES), f32),
            jax.ShapeDtypeStruct((8, LANES), f32),
        ),
        in_specs=[smem, smem, smem, vmem, vmem],
        out_specs=(vmem, vmem, vmem),
        scratch_shapes=[pltpu.VMEM((5, NY * 32, LANES), f32)],
        name="block",
        compiler_params=SMALL,
    )(bucket, scale, fix, first, second)


def adam_kernel(grad_ref, row_ref, master_ref, one_ref, two_ref, master_out, one_out, two_out, half_out):
    pieces = []
    for x in range(NX):
        g = grad_ref[x, 0].astype(f32)
        tail = g[32:40]
        pieces.append(g[:32])
        pieces.append(jnp.concatenate([tail[:, 32 * k : 32 * k + 32] for k in range(4)], axis=0))
    grad = jnp.concatenate(pieces, axis=1)
    commit = row_ref[0:1, :] == 0.0
    master, one, two = master_ref[...], one_ref[...], two_ref[...]
    new, first, second = update(master, one, two, grad, row_ref[1:2, :], row_ref[2:3, :])
    master = jnp.where(commit, new, master)
    master_out[...] = master
    half_out[...] = master.astype(bf16)
    one_out[...] = jnp.where(commit, first, one)
    two_out[...] = jnp.where(commit, second, two)


def adam(grad, row, master, one, two):
    rows, width = master.shape
    step = width // NY
    full = pl.BlockSpec((rows, step), lambda i: (0, i))
    return pl.pallas_call(
        adam_kernel,
        out_shape=(*[jax.ShapeDtypeStruct(master.shape, f32)] * 3, jax.ShapeDtypeStruct(master.shape, bf16)),
        grid=(NY,),
        in_specs=[
            pl.BlockSpec((NX, 1, 40, LANES), lambda i: (0, i, 0, 0)),
            pl.BlockSpec((8, step), lambda i: (0, i)),
            full,
            full,
            full,
        ],
        out_specs=(full, full, full, full),
        name="adam",
        compiler_params=SMALL,
    )(grad.reshape(NX, NY, 40, LANES), row, master, one, two)


def local(tokens, out_grad, master, moment_one, moment_two, flags, steps, rate):
    rows, width = master.shape
    bucket_width = width // BUCKETS
    ix, iy = lax.axis_index("x"), lax.axis_index("y")

    times = (steps + 1).astype(f32)
    scales = rate[0] / (1.0 - jnp.power(f32(first_decay), times))
    fixes = 1.0 / (1.0 - jnp.power(f32(second_decay), times))
    bucket = ((iy * NX + ix) // 2)[None]

    mine = jnp.pad(flags.astype(f32), ((0, 7), (0, LANES - BUCKETS)))
    first = exchange(pack(ix[None], tokens.T, mine, master, moment_one, moment_two), XY)

    perm = [(zh * NX + x, x * NX + zh) for zh in range(NX) for x in range(NX)]
    og = lax.ppermute(out_grad.T, ("zh", "x"), perm)
    seen = jnp.max(first[:, 72:80, :], axis=0)
    og = jnp.concatenate([og, seen], axis=0)
    second = exchange(jnp.broadcast_to(og[None], (NZC, *og.shape)), ZC)

    grad, part, count = block(bucket, scales, fixes, first, second)
    total = jnp.sum(exchange(part, ZC), axis=0)
    result = lax.ppermute(total.astype(bf16), ("zh", "x"), perm).T
    grad = exchange(grad, XY)

    counts = count[0, :BUCKETS]
    row = jnp.stack([counts, scales, fixes, *[counts] * 5])
    row = jnp.repeat(row, bucket_width, axis=1)
    master_next, one_next, two_next, half = adam(grad, row, master, moment_one, moment_two)
    steps_next = steps + (counts == 0).astype(jnp.int32)
    return master_next, one_next, two_next, half, steps_next, result


def solution(mesh):
    split = Mesh(mesh.devices.reshape(8, 4, 2, 2, 4), ALL)
    in_specs = (P("x", FSDP), P("x", FSDP), P(FSDP), P(FSDP), P(FSDP), P(ALL), P(), P())
    out_specs = (P(FSDP), P(FSDP), P(FSDP), P(FSDP), P(), P("x", FSDP))
    return jax.shard_map(local, mesh=split, in_specs=in_specs, out_specs=out_specs, check_vma=False)
```

time: 145 us -> 98.1 us (0.68)
  the two profiles are of different devices: /device:TPU:5 before, /device:TPU:8 now
where the time goes in v2:
time: 98.1 us; the launch traced here: 97.6 us
  waiting for transfers between devices  41.3 us (42%)
  starting transfers between devices  27.2 us (28%)
  blocking collectives  15.6 us (16%)
  Pallas kernels  8.08 us (8%)
  local copies, waits for them, and re-layouts  3.43 us (3%)
  between operations  1.41 us (1%)
    all_to_all x3, waiting for transfers between devices, exchange(): return lax.all_to_all(x, axes, 0, 0, tiled=True)  41.3 us
    all_to_all x3, starting transfers between devices, exchange(): return lax.all_to_all(x, axes, 0, 0, tiled=True)  25.9 us
    all_to_all x1, blocking collectives, exchange(): return lax.all_to_all(x, axes, 0, 0, tiled=True)  15.6 us
    pallas_call x1, Pallas kernels, adam(): pl.pallas_call(adam_kernel, out_shape=(*[jax.ShapeDtypeStruct(master.shap...  3.88 us
    pallas_call x1, Pallas kernels, pack(): pl.pallas_call(pack_kernel, out_shape=jax.ShapeDtypeStruct((NX * NY, 80,...  2.18 us
    pallas_call x1, Pallas kernels, block(): pl.pallas_call(block_kernel, out_shape=(jax.ShapeDtypeStruct((NX * NY, 40...  2.02 us
  transfers between devices with their start and end apart: 5, of which 3 were waited for; matrix products, arithmetic and copies ran while one was open for 1% of the time, Pallas kernels for 0%

profile of v2, /device:TPU:8, one launch (start us, length us, event | category | flops | bytes accessed | tf_op | source)
XLA Modules:
  0.0 97.6 jit_solution(15348028145038953952)
XLA Ops:
  0.6 0.6 copy-done.5
  1.3 0.6 pad.4.flag_ref
  1.9 2.2 %pack.1 = bf16[32,80,128]{2,1,0:T(8,128)(2,1)} custom-call(s32[1]{0:T(128)} %bitcast.2.ix_ref, bf16[32,128]{1,0:T(8,128)(2,1)} %bitcast.18, f32[8,128]{1,0:T(8,128)} %pad.4.flag_ref, f32[32,5120]{1,0:T(8,128)} %master_ref.3, f32[32,5120]{1,0:T(8,128)} %one_ref.3, f32[32,5120]{1,0:T(8,128)} %two_ref.3), custom_call_target="tpu_custom_call" | custom-call | tf_op jit(solution)/shard_map/pack/pallas_call | solution.py:50
  4.1 10.3 %all-to-all-start = ((bf16[32,80,128]{2,1,0:T(8,128)(2,1)}), bf16[32,80,128]{2,1,0:T(8,128)(2,1)S(1)}, u32[]{:S(2)}, u32[]{:S(2)}) async-start(bf16[32,80,128]{2,1,0:T(8,128)(2,1)} %pack.1), calls=%async_computation | async-start | bytes 1310720 | tf_op jit(solution)/shard_map/all_to_all | solution.py:25
  14.4 0.0 copy-done.4
  14.4 0.7 collective-permute-start
  15.1 19.6 %all-to-all-done.first_ref = bf16[32,80,128]{2,1,0:T(8,128)(2,1)S(1)} async-done(((bf16[32,80,128]{2,1,0:T(8,128)(2,1)}), bf16[32,80,128]{2,1,0:T(8,128)(2,1)S(1)}, u32[]{:S(2)}, u32[]{:S(2)}) %all-to-all-start) | async-done | bytes 655392 | tf_op jit(solution)/shard_map/all_to_all | solution.py:25
  34.7 0.0 collective-permute-done
  34.7 0.7 broadcast_in_dim.17
  35.4 10.4 %all-to-all-start.1 = ((bf16[16,48,128]{2,1,0:T(8,128)(2,1)}), bf16[16,48,128]{2,1,0:T(8,128)(2,1)S(1)}, u32[]{:S(2)}, u32[]{:S(2)}) async-start(bf16[16,48,128]{2,1,0:T(8,128)(2,1)} %broadcast_in_dim.17), calls=%async_computation.1 | async-start | bytes 393216 | tf_op jit(solution)/shard_map/all_to_all | solution.py:25
  46.5 0.0 copy-start.3
  46.5 0.6 copy-done.3
  47.2 8.5 %all-to-all-done.1.second_ref = bf16[16,48,128]{2,1,0:T(8,128)(2,1)S(1)} async-done(((bf16[16,48,128]{2,1,0:T(8,128)(2,1)}), bf16[16,48,128]{2,1,0:T(8,128)(2,1)S(1)}, u32[]{:S(2)}, u32[]{:S(2)}) %all-to-all-start.1) | async-done | bytes 196640 | tf_op jit(solution)/shard_map/all_to_all | solution.py:25
  55.7 2.0 %block.1 = (bf16[32,40,128]{2,1,0:T(8,128)(2,1)}, f32[16,40,128]{2,1,0:T(8,128)S(1)}, f32[8,128]{1,0:T(8,128)S(1)}) custom-call(s32[1]{0:T(128)} %bitcast.bucket_ref, f32[16]{0:T(128)S(1)} %get-tuple-element.21.scale_ref, f32[16]{0:T(128)S(1)} %get-tuple-element.20.fix_ref, bf16[32,80,128]{2,1,0:T(8,128)(2,1)S(1)} %all-to-all-done.first_ref, ...), custom_call_target="tpu_custom_call" | custom-call | tf_op jit(solution)/shard_map/block/pallas_call | solution.py:113
  57.7 15.6 %all_to_all.20 = f32[16,40,128]{2,1,0:T(8,128)S(1)} all-to-all(f32[16,40,128]{2,1,0:T(8,128)S(1)} %get-tuple-element.19), channel_id=1, replica_groups=mesh['y'=8,'zh'=4,'zl'=2,'c'=2,'x'=4] {'zh','zl','c'}, dimensions={0} | all-to-all | bytes 655360 | tf_op jit(solution)/shard_map/all_to_all | solution.py:25
  73.3 5.2 %all-to-all-start.2 = ((bf16[32,40,128]{2,1,0:T(8,128)(2,1)}), bf16[32,40,128]{2,1,0:T(8,128)(2,1)S(1)}, u32[]{:S(2)}, u32[]{:S(2)}) async-start(bf16[32,40,128]{2,1,0:T(8,128)(2,1)} %get-tuple-element.13), calls=%async_computation.2 | async-start | bytes 655360 | tf_op jit(solution)/shard_map/all_to_all | solution.py:25
  78.5 0.7 collective-permute-start.1
  79.2 0.5 fusion.1
  79.7 0.1 broadcast_in_dim.18
  79.8 0.1 reshape.24.row_ref
  79.9 0.0 collective-permute-done.1
  79.9 13.2 %all-to-all-done.2 = bf16[32,40,128]{2,1,0:T(8,128)(2,1)S(1)} async-done(((bf16[32,40,128]{2,1,0:T(8,128)(2,1)}), bf16[32,40,128]{2,1,0:T(8,128)(2,1)S(1)}, u32[]{:S(2)}, u32[]{:S(2)}) %all-to-all-start.2) | async-done | bytes 327712 | tf_op jit(solution)/shard_map/all_to_all | solution.py:25
  93.1 3.9 %adam.1 = (f32[32,5120]{1,0:T(8,128)}, f32[32,5120]{1,0:T(8,128)}, f32[32,5120]{1,0:T(8,128)}, bf16[32,5120]{1,0:T(8,128)(2,1)}) custom-call(bf16[4,8,40,128]{3,2,1,0:T(8,128)(2,1)S(1)} %bitcast.14, f32[8,5120]{1,0:T(8,128)S(1)} %reshape.24.row_ref, f32[32,5120]{1,0:T(8,128)S(1)} %copy-done, f32[32,5120]{1,0:T(8,128)S(1)} %copy-done.1, f32[32,5120]{1,0:T(8,128)S(1)} %copy-done.2), custom_call_target="tpu_custom_call" | custom-call | tf_op jit(solution)/shard_map/adam/pallas_call | solution.py:150
  97.0 0.6 copy.16
  (15 shorter events, 0.1 us)
Async XLA Ops:
  0.6 0.7 copy-start.5
  4.1 10.3 %copy-start.4 = (bf16[128,40]{0,1:T(8,128)(2,1)S(1)}, bf16[128,40]{0,1:T(8,128)(2,1)}, u32[]{:S(2)}) copy-start(bf16[128,40]{0,1:T(8,128)(2,1)} %param.9) | copy-start | bytes 30724
  4.1 30.6 %all-to-all-start = ((bf16[32,80,128]{2,1,0:T(8,128)(2,1)}), bf16[32,80,128]{2,1,0:T(8,128)(2,1)S(1)}, u32[]{:S(2)}, u32[]{:S(2)}) async-start(bf16[32,80,128]{2,1,0:T(8,128)(2,1)} %pack.1), calls=%async_computation | async-start | bytes 1310720 | tf_op jit(solution)/shard_map/all_to_all | solution.py:25
  14.4 20.3 %collective-permute-start = (bf16[40,128]{1,0:T(8,128)(2,1)S(1)}, bf16[40,128]{1,0:T(8,128)(2,1)S(1)}, u32[]{:S(2)}, u32[]{:S(2)}) collective-permute-start(bf16[40,128]{1,0:T(8,128)(2,1)S(1)} %bitcast.19), channel_id=1, source_target_pairs={{0,0},{1,16},{2,32},{3,48},{16,1},{17,17},{18,33},{19,49},{32,2},{... | collective-permute-start | bytes 30728 | tf_op jit(solution)/shard_map/ppermute | solution.py:181
  35.4 20.3 %all-to-all-start.1 = ((bf16[16,48,128]{2,1,0:T(8,128)(2,1)}), bf16[16,48,128]{2,1,0:T(8,128)(2,1)S(1)}, u32[]{:S(2)}, u32[]{:S(2)}) async-start(bf16[16,48,128]{2,1,0:T(8,128)(2,1)} %broadcast_in_dim.17), calls=%async_computation.1 | async-start | bytes 393216 | tf_op jit(solution)/shard_map/all_to_all | solution.py:25
  46.5 0.7 copy-start.3
  57.7 35.4 %copy-start.2 = (f32[32,5120]{1,0:T(8,128)S(1)}, f32[32,5120]{1,0:T(8,128)}, u32[]{:S(2)}) copy-start(f32[32,5120]{1,0:T(8,128)} %two_ref.3) | copy-start | bytes 1966084
  73.3 19.8 %copy-start = (f32[32,5120]{1,0:T(8,128)S(1)}, f32[32,5120]{1,0:T(8,128)}, u32[]{:S(2)}) copy-start(f32[32,5120]{1,0:T(8,128)} %master_ref.3) | copy-start | bytes 1966084
  73.3 19.8 %copy-start.1 = (f32[32,5120]{1,0:T(8,128)S(1)}, f32[32,5120]{1,0:T(8,128)}, u32[]{:S(2)}) copy-start(f32[32,5120]{1,0:T(8,128)} %one_ref.3) | copy-start | bytes 1966084
  73.3 19.8 %all-to-all-start.2 = ((bf16[32,40,128]{2,1,0:T(8,128)(2,1)}), bf16[32,40,128]{2,1,0:T(8,128)(2,1)S(1)}, u32[]{:S(2)}, u32[]{:S(2)}) async-start(bf16[32,40,128]{2,1,0:T(8,128)(2,1)} %get-tuple-element.13), calls=%async_computation.2 | async-start | bytes 655360 | tf_op jit(solution)/shard_map/all_to_all | solution.py:25
  78.5 1.4 %collective-permute-start.1 = (bf16[40,128]{1,0:T(8,128)(2,1)S(1)}, bf16[40,128]{1,0:T(8,128)(2,1)S(1)}, u32[]{:S(2)}, u32[]{:S(2)}) collective-permute-start(bf16[40,128]{1,0:T(8,128)(2,1)S(1)} %reduce_sum.9), channel_id=1, source_target_pairs={{0,0},{1,16},{2,32},{3,48},{16,1},{17,17},{18,33},{19,49},{32,2},{... | collective-permute-start | bytes 30728 | tf_op jit(solution)/shard_map/ppermute | solution.py:188

commit v3 on v2

--- a/solution.py
+++ b/solution.py
@@ -26,21 +26,24 @@
 
 
 def pack_kernel(ix_ref, tok_ref, flag_ref, master_ref, one_ref, two_ref, out_ref):
+    flag = jnp.concatenate([flag_ref[...].astype(f32), jnp.zeros((1, LANES - BUCKETS), f32)], axis=1)
+    flag = jnp.broadcast_to(flag, (8, LANES))
     tok = tok_ref[...]
-    flag = flag_ref[...]
-    master = master_ref[...]
-    high = master.astype(bf16).astype(f32)
-    parts = (high, master - high, one_ref[...], two_ref[...])
-    for x in range(NX):
-        for y in range(NY):
-            c = (y * NX + x) * 160
-            d = x * NY + y
-            out_ref[d, 0:32, :] = tok
-            main = [p[:, c : c + LANES] for p in parts]
-            rest = jnp.concatenate([p[:, c + LANES : c + 160] for p in parts], axis=1)
-            out_ref[d, 32:48, :] = jnp.concatenate(main[:2], axis=0).astype(bf16)
-            out_ref[d, 48:64, :] = jnp.concatenate(main[2:], axis=0).astype(bf16)
-            out_ref[d, 64:80, :] = jnp.concatenate([rest, flag], axis=0).astype(bf16)
+    for x in range(NX):
+
+        @pl.when(pl.program_id(0) == x)
+        def _():
+            for y in range(NY):
+                c = (y * NX + x) * 160
+                master = master_ref[:, c : c + 160]
+                high = master.astype(bf16).astype(f32)
+                parts = (high, master - high, one_ref[:, c : c + 160], two_ref[:, c : c + 160])
+                main = [p[:, :LANES] for p in parts]
+                rest = jnp.concatenate([p[:, LANES:] for p in parts], axis=1)
+                out_ref[y, 0:32, :] = tok
+                out_ref[y, 32:48, :] = jnp.concatenate(main[:2], axis=0).astype(bf16)
+                out_ref[y, 48:64, :] = jnp.concatenate(main[2:], axis=0).astype(bf16)
+                out_ref[y, 64:80, :] = jnp.concatenate([rest, flag], axis=0).astype(bf16)
 
 
 def pack(ix, tok, flag, master, one, two):
@@ -52,9 +55,9 @@
         out_shape=jax.ShapeDtypeStruct((NX * NY, 80, LANES), bf16),
         grid_spec=pltpu.PrefetchScalarGridSpec(
             num_scalar_prefetch=1,
-            grid=(1,),
+            grid=(NX,),
             in_specs=[whole(tok), whole(flag), part, part, part],
-            out_specs=pl.BlockSpec((NX * NY, 80, LANES), lambda i, ix: (0, 0, 0)),
+            out_specs=pl.BlockSpec((NY, 80, LANES), lambda i, ix: (i, 0, 0)),
         ),
         name="pack",
     )(ix, tok, flag, master, one, two)
@@ -105,7 +108,7 @@
     for x in range(NX):
         out = jnp.dot(weight, tok[x], preferred_element_type=f32)
         for k in range(NX):
-            part_ref[x * NX + k] = out[40 * k : 40 * k + 40, :]
+            part_ref[x * NX + k] = out[40 * k : 40 * k + 40, :].astype(bf16)
 
 
 def block(bucket, scale, fix, first, second):
@@ -114,7 +117,7 @@
         block_kernel,
         out_shape=(
             jax.ShapeDtypeStruct((NX * NY, 40, LANES), bf16),
-            jax.ShapeDtypeStruct((NZC, 40, LANES), f32),
+            jax.ShapeDtypeStruct((NZC, 40, LANES), bf16),
             jax.ShapeDtypeStruct((8, LANES), f32),
         ),
         in_specs=[smem, smem, smem, vmem, vmem],
@@ -125,17 +128,21 @@
     )(bucket, scale, fix, first, second)
 
 
-def adam_kernel(grad_ref, row_ref, master_ref, one_ref, two_ref, master_out, one_out, two_out, half_out):
+def adam_kernel(grad_ref, row_ref, result_ref, master_ref, one_ref, two_ref, master_out, one_out, two_out, half_out, result_out):
+    step = master_out.shape[1]
+    i = pl.program_id(0)
+    here = pl.ds(pl.multiple_of(i * step, LANES), step)
+    result_out[...] = result_ref[...]
     pieces = []
     for x in range(NX):
-        g = grad_ref[x, 0].astype(f32)
+        g = grad_ref[x, i].astype(f32)
         tail = g[32:40]
         pieces.append(g[:32])
         pieces.append(jnp.concatenate([tail[:, 32 * k : 32 * k + 32] for k in range(4)], axis=0))
     grad = jnp.concatenate(pieces, axis=1)
-    commit = row_ref[0:1, :] == 0.0
-    master, one, two = master_ref[...], one_ref[...], two_ref[...]
-    new, first, second = update(master, one, two, grad, row_ref[1:2, :], row_ref[2:3, :])
+    commit = row_ref[0:1, here] == 0.0
+    master, one, two = master_ref[:, here], one_ref[:, here], two_ref[:, here]
+    new, first, second = update(master, one, two, grad, row_ref[1:2, here], row_ref[2:3, here])
     master = jnp.where(commit, new, master)
     master_out[...] = master
     half_out[...] = master.astype(bf16)
@@ -143,25 +150,24 @@
     two_out[...] = jnp.where(commit, second, two)
 
 
-def adam(grad, row, master, one, two):
+def adam(grad, row, result, master, one, two):
     rows, width = master.shape
     step = width // NY
     full = pl.BlockSpec((rows, step), lambda i: (0, i))
+    vmem = pl.BlockSpec(memory_space=VMEM)
     return pl.pallas_call(
         adam_kernel,
-        out_shape=(*[jax.ShapeDtypeStruct(master.shape, f32)] * 3, jax.ShapeDtypeStruct(master.shape, bf16)),
+        out_shape=(
+            *[jax.ShapeDtypeStruct(master.shape, f32)] * 3,
+            jax.ShapeDtypeStruct(master.shape, bf16),
+            jax.ShapeDtypeStruct(result.shape, bf16),
+        ),
         grid=(NY,),
-        in_specs=[
-            pl.BlockSpec((NX, 1, 40, LANES), lambda i: (0, i, 0, 0)),
-            pl.BlockSpec((8, step), lambda i: (0, i)),
-            full,
-            full,
-            full,
-        ],
-        out_specs=(full, full, full, full),
+        in_specs=[vmem] * 6,
+        out_specs=(full, full, full, full, pl.BlockSpec(result.shape, lambda i: (0, 0))),
         name="adam",
         compiler_params=SMALL,
-    )(grad.reshape(NX, NY, 40, LANES), row, master, one, two)
+    )(grad.reshape(NX, NY, 40, LANES), row, result, master, one, two)
 
 
 def local(tokens, out_grad, master, moment_one, moment_two, flags, steps, rate):
@@ -174,8 +180,7 @@
     fixes = 1.0 / (1.0 - jnp.power(f32(second_decay), times))
     bucket = ((iy * NX + ix) // 2)[None]
 
-    mine = jnp.pad(flags.astype(f32), ((0, 7), (0, LANES - BUCKETS)))
-    first = exchange(pack(ix[None], tokens.T, mine, master, moment_one, moment_two), XY)
+    first = exchange(pack(ix[None], tokens.T, flags, master, moment_one, moment_two), XY)
 
     perm = [(zh * NX + x, x * NX + zh) for zh in range(NX) for x in range(NX)]
     og = lax.ppermute(out_grad.T, ("zh", "x"), perm)
@@ -184,16 +189,16 @@
     second = exchange(jnp.broadcast_to(og[None], (NZC, *og.shape)), ZC)
 
     grad, part, count = block(bucket, scales, fixes, first, second)
-    total = jnp.sum(exchange(part, ZC), axis=0)
-    result = lax.ppermute(total.astype(bf16), ("zh", "x"), perm).T
+    total = jnp.sum(exchange(part, ZC).astype(f32), axis=0)
+    result = lax.ppermute(total.astype(bf16), ("zh", "x"), perm)
     grad = exchange(grad, XY)
 
     counts = count[0, :BUCKETS]
     row = jnp.stack([counts, scales, fixes, *[counts] * 5])
     row = jnp.repeat(row, bucket_width, axis=1)
-    master_next, one_next, two_next, half = adam(grad, row, master, moment_one, moment_two)
+    master_next, one_next, two_next, half, result = adam(grad, row, result, master, moment_one, moment_two)
     steps_next = steps + (counts == 0).astype(jnp.int32)
-    return master_next, one_next, two_next, half, steps_next, result
+    return master_next, one_next, two_next, half, steps_next, result.T
 
 
 def solution(mesh):

time: 98.1 us -> 93.2 us (0.950)
  blocking collectives: 15.6 us -> 12.3 us
  local copies, waits for them, and re-layouts: 3.43 us -> 1.59 us
    all_to_all x1, blocking collectives: 15.6 us -> 12.3 us  [exchange(): return lax.all_to_all(x, axes, 0, 0, tiled=True)]
    unnamed x13 -> x10, local copies, waits for them, and re-layouts: 1.91 us -> 0.67 us
where the time goes in v3:
time: 93.2 us; the launch traced here: 92.7 us
  waiting for transfers between devices  41 us (44%)
  starting transfers between devices  27.2 us (29%)
  blocking collectives  12.3 us (13%)
  Pallas kernels  8.63 us (9%)
  local copies, waits for them, and re-layouts  1.59 us (2%)
  between operations  1.4 us (2%)
    all_to_all x3, waiting for transfers between devices, exchange(): return lax.all_to_all(x, axes, 0, 0, tiled=True)  41 us
    all_to_all x3, starting transfers between devices, exchange(): return lax.all_to_all(x, axes, 0, 0, tiled=True)  25.9 us
    all_to_all x1, blocking collectives, exchange(): return lax.all_to_all(x, axes, 0, 0, tiled=True)  12.3 us
    pallas_call x1, Pallas kernels, adam(): pl.pallas_call(adam_kernel, out_shape=(*[jax.ShapeDtypeStruct(master.shap...  3.73 us
    pallas_call x1, Pallas kernels, pack(): pl.pallas_call(pack_kernel, out_shape=jax.ShapeDtypeStruct((NX * NY, 80,...  2.88 us
    pallas_call x1, Pallas kernels, block(): pl.pallas_call(block_kernel, out_shape=(jax.ShapeDtypeStruct((NX * NY, 40...  2.02 us
  transfers between devices with their start and end apart: 5, of which 3 were waited for; matrix products, arithmetic and copies ran while one was open for 1% of the time, Pallas kernels for 0%

profile of v3, /device:TPU:8, one launch (start us, length us, event | category | flops | bytes accessed | tf_op | source)
XLA Modules:
  0.0 92.7 jit_solution(6170167913520253438)
XLA Ops:
  0.6 2.9 %pack.1 = bf16[32,80,128]{2,1,0:T(8,128)(2,1)} custom-call(s32[1]{0:T(128)} %bitcast.2.ix_ref, bf16[32,128]{1,0:T(8,128)(2,1)} %bitcast.17, s32[1,16]{1,0:T(1,128)} %flag_ref.1, f32[32,5120]{1,0:T(8,128)} %master_ref.3, f32[32,5120]{1,0:T(8,128)} %one_ref.3, f32[32,5120]{1,0:T(8,128)} %two_ref.3), custom_call_target="tpu_custom_call" | custom-call | tf_op jit(solution)/shard_map/pack/pallas_call | solution.py:53
  3.5 10.3 %all-to-all-start = ((bf16[32,80,128]{2,1,0:T(8,128)(2,1)}), bf16[32,80,128]{2,1,0:T(8,128)(2,1)S(1)}, u32[]{:S(2)}, u32[]{:S(2)}) async-start(bf16[32,80,128]{2,1,0:T(8,128)(2,1)} %pack.1), calls=%async_computation | async-start | bytes 1310720 | tf_op jit(solution)/shard_map/all_to_all | solution.py:25
  13.8 0.0 copy-done.4
  13.8 0.7 collective-permute-start
  14.5 19.6 %all-to-all-done.first_ref = bf16[32,80,128]{2,1,0:T(8,128)(2,1)S(1)} async-done(((bf16[32,80,128]{2,1,0:T(8,128)(2,1)}), bf16[32,80,128]{2,1,0:T(8,128)(2,1)S(1)}, u32[]{:S(2)}, u32[]{:S(2)}) %all-to-all-start) | async-done | bytes 655392 | tf_op jit(solution)/shard_map/all_to_all | solution.py:25
  34.1 0.0 collective-permute-done
  34.1 0.7 broadcast_in_dim.17
  34.8 10.4 %all-to-all-start.1 = ((bf16[16,48,128]{2,1,0:T(8,128)(2,1)}), bf16[16,48,128]{2,1,0:T(8,128)(2,1)S(1)}, u32[]{:S(2)}, u32[]{:S(2)}) async-start(bf16[16,48,128]{2,1,0:T(8,128)(2,1)} %broadcast_in_dim.17), calls=%async_computation.1 | async-start | bytes 393216 | tf_op jit(solution)/shard_map/all_to_all | solution.py:25
  45.9 0.0 copy-start.3
  45.9 0.6 copy-done.3
  46.6 8.5 %all-to-all-done.1.second_ref = bf16[16,48,128]{2,1,0:T(8,128)(2,1)S(1)} async-done(((bf16[16,48,128]{2,1,0:T(8,128)(2,1)}), bf16[16,48,128]{2,1,0:T(8,128)(2,1)S(1)}, u32[]{:S(2)}, u32[]{:S(2)}) %all-to-all-start.1) | async-done | bytes 196640 | tf_op jit(solution)/shard_map/all_to_all | solution.py:25
  55.2 2.0 %block.1 = (bf16[32,40,128]{2,1,0:T(8,128)(2,1)}, bf16[16,40,128]{2,1,0:T(8,128)(2,1)S(1)}, f32[8,128]{1,0:T(8,128)S(1)}) custom-call(s32[1]{0:T(128)} %bitcast.bucket_ref, f32[16]{0:T(128)S(1)} %get-tuple-element.23.scale_ref, f32[16]{0:T(128)S(1)} %get-tuple-element.22.fix_ref, bf16[32,80,128]{2,1,0:T(8,128)(2,1)S(1)} %all-to-all-done.first_ref, ...), custom_call_target="tpu_custom_call" | custom-call | tf_op jit(solution)/shard_map/block/pallas_call | solution.py:116
  57.2 12.3 %all_to_all.20 = bf16[16,40,128]{2,1,0:T(8,128)(2,1)S(1)} all-to-all(bf16[16,40,128]{2,1,0:T(8,128)(2,1)S(1)} %get-tuple-element.16), channel_id=1, replica_groups=mesh['y'=8,'zh'=4,'zl'=2,'c'=2,'x'=4] {'zh','zl','c'}, dimensions={0} | all-to-all | bytes 327680 | tf_op jit(solution)/shard_map/all_to_all | solution.py:25
  69.4 5.2 %all-to-all-start.2 = ((bf16[32,40,128]{2,1,0:T(8,128)(2,1)}), bf16[32,40,128]{2,1,0:T(8,128)(2,1)S(1)}, u32[]{:S(2)}, u32[]{:S(2)}) async-start(bf16[32,40,128]{2,1,0:T(8,128)(2,1)} %get-tuple-element.14), calls=%async_computation.2 | async-start | bytes 655360 | tf_op jit(solution)/shard_map/all_to_all | solution.py:25
  74.6 0.7 collective-permute-start.1
  75.3 0.5 fusion.1
  75.9 0.1 broadcast_in_dim.18
  76.0 0.1 reshape.24.row_ref
  76.1 0.0 collective-permute-done.1.result_ref
  76.1 12.9 %all-to-all-done.2 = bf16[32,40,128]{2,1,0:T(8,128)(2,1)S(1)} async-done(((bf16[32,40,128]{2,1,0:T(8,128)(2,1)}), bf16[32,40,128]{2,1,0:T(8,128)(2,1)S(1)}, u32[]{:S(2)}, u32[]{:S(2)}) %all-to-all-start.2) | async-done | bytes 327712 | tf_op jit(solution)/shard_map/all_to_all | solution.py:25
  89.0 0.0 copy-done.2
  89.0 0.0 copy-done
  89.0 0.0 copy-done.1
  89.0 3.7 %adam.1 = (f32[32,5120]{1,0:T(8,128)}, f32[32,5120]{1,0:T(8,128)}, f32[32,5120]{1,0:T(8,128)}, bf16[32,5120]{1,0:T(8,128)(2,1)}, bf16[40,128]{1,0:T(8,128)(2,1)}) custom-call(bf16[4,8,40,128]{3,2,1,0:T(8,128)(2,1)S(1)} %bitcast.14, f32[8,5120]{1,0:T(8,128)S(1)} %reshape.24.row_ref, bf16[40,128]{1,0:T(8,128)(2,1)S(1)} %collective-permute-done.1.result_ref, ...), custom_call_target="tpu_custom_call" | custom-call | tf_op jit(solution)/shard_map/adam/pallas_call | solution.py:158
  (10 shorter events, 0.1 us)
Async XLA Ops:
  3.5 10.3 %copy-start.4 = (bf16[128,40]{0,1:T(8,128)(2,1)S(1)}, bf16[128,40]{0,1:T(8,128)(2,1)}, u32[]{:S(2)}) copy-start(bf16[128,40]{0,1:T(8,128)(2,1)} %param.9) | copy-start | bytes 30724
  3.5 30.6 %all-to-all-start = ((bf16[32,80,128]{2,1,0:T(8,128)(2,1)}), bf16[32,80,128]{2,1,0:T(8,128)(2,1)S(1)}, u32[]{:S(2)}, u32[]{:S(2)}) async-start(bf16[32,80,128]{2,1,0:T(8,128)(2,1)} %pack.1), calls=%async_computation | async-start | bytes 1310720 | tf_op jit(solution)/shard_map/all_to_all | solution.py:25
  13.8 20.3 %collective-permute-start = (bf16[40,128]{1,0:T(8,128)(2,1)S(1)}, bf16[40,128]{1,0:T(8,128)(2,1)S(1)}, u32[]{:S(2)}, u32[]{:S(2)}) collective-permute-start(bf16[40,128]{1,0:T(8,128)(2,1)S(1)} %bitcast.18), channel_id=1, source_target_pairs={{0,0},{1,16},{2,32},{3,48},{16,1},{17,17},{18,33},{19,49},{32,2},{... | collective-permute-start | bytes 30728 | tf_op jit(solution)/shard_map/ppermute | solution.py:186
  34.8 20.3 %all-to-all-start.1 = ((bf16[16,48,128]{2,1,0:T(8,128)(2,1)}), bf16[16,48,128]{2,1,0:T(8,128)(2,1)S(1)}, u32[]{:S(2)}, u32[]{:S(2)}) async-start(bf16[16,48,128]{2,1,0:T(8,128)(2,1)} %broadcast_in_dim.17), calls=%async_computation.1 | async-start | bytes 393216 | tf_op jit(solution)/shard_map/all_to_all | solution.py:25
  45.9 0.7 copy-start.3
  55.2 33.8 %copy-start.2 = (f32[32,5120]{1,0:T(8,128)S(1)}, f32[32,5120]{1,0:T(8,128)}, u32[]{:S(2)}) copy-start(f32[32,5120]{1,0:T(8,128)} %two_ref.3) | copy-start | bytes 1966084
  69.4 19.5 %copy-start = (f32[32,5120]{1,0:T(8,128)S(1)}, f32[32,5120]{1,0:T(8,128)}, u32[]{:S(2)}) copy-start(f32[32,5120]{1,0:T(8,128)} %master_ref.3) | copy-start | bytes 1966084
  69.4 19.5 %copy-start.1 = (f32[32,5120]{1,0:T(8,128)S(1)}, f32[32,5120]{1,0:T(8,128)}, u32[]{:S(2)}) copy-start(f32[32,5120]{1,0:T(8,128)} %one_ref.3) | copy-start | bytes 1966084
  69.4 19.5 %all-to-all-start.2 = ((bf16[32,40,128]{2,1,0:T(8,128)(2,1)}), bf16[32,40,128]{2,1,0:T(8,128)(2,1)S(1)}, u32[]{:S(2)}, u32[]{:S(2)}) async-start(bf16[32,40,128]{2,1,0:T(8,128)(2,1)} %get-tuple-element.14), calls=%async_computation.2 | async-start | bytes 655360 | tf_op jit(solution)/shard_map/all_to_all | solution.py:25
  74.6 1.4 %collective-permute-start.1 = (bf16[40,128]{1,0:T(8,128)(2,1)S(1)}, bf16[40,128]{1,0:T(8,128)(2,1)S(1)}, u32[]{:S(2)}, u32[]{:S(2)}) collective-permute-start(bf16[40,128]{1,0:T(8,128)(2,1)S(1)} %reduce_sum.12), channel_id=1, source_target_pairs={{0,0},{1,16},{2,32},{3,48},{16,1},{17,17},{18,33},{19,49},{32,2},{... | collective-permute-start | bytes 30728 | tf_op jit(solution)/shard_map/ppermute | solution.py:193

commit v4 on v3

--- a/solution.py
+++ b/solution.py
@@ -12,7 +12,9 @@
 ZC = ("zh", "zl", "c")
 XY = ("x", "y")
 NX, NY, NZC = 4, 8, 16
+STEPS = 4
 LANES = 128
+FLAGS = 96
 first_decay = 0.9
 second_decay = 0.95
 epsilon = 1e-08
@@ -26,24 +28,19 @@
 
 
 def pack_kernel(ix_ref, tok_ref, flag_ref, master_ref, one_ref, two_ref, out_ref):
-    flag = jnp.concatenate([flag_ref[...].astype(f32), jnp.zeros((1, LANES - BUCKETS), f32)], axis=1)
-    flag = jnp.broadcast_to(flag, (8, LANES))
+    flag = jnp.concatenate([flag_ref[...].astype(f32), jnp.zeros((1, 32 - BUCKETS), f32)], axis=1)
+    flag = jnp.broadcast_to(flag, (8, 32))
     tok = tok_ref[...]
     for x in range(NX):
-
-        @pl.when(pl.program_id(0) == x)
-        def _():
-            for y in range(NY):
-                c = (y * NX + x) * 160
-                master = master_ref[:, c : c + 160]
-                high = master.astype(bf16).astype(f32)
-                parts = (high, master - high, one_ref[:, c : c + 160], two_ref[:, c : c + 160])
-                main = [p[:, :LANES] for p in parts]
-                rest = jnp.concatenate([p[:, LANES:] for p in parts], axis=1)
-                out_ref[y, 0:32, :] = tok
-                out_ref[y, 32:48, :] = jnp.concatenate(main[:2], axis=0).astype(bf16)
-                out_ref[y, 48:64, :] = jnp.concatenate(main[2:], axis=0).astype(bf16)
-                out_ref[y, 64:80, :] = jnp.concatenate([rest, flag], axis=0).astype(bf16)
+        for y in range(NY):
+            c = (y * NX + x) * 160
+            d = x * NY + y
+            parts = [p[:, c : c + 160] for p in (master_ref, one_ref, two_ref)]
+            main = [p[:, :LANES] for p in parts]
+            rest = jnp.concatenate([p[:, LANES:] for p in parts] + [flag], axis=1)
+            out_ref[d, 0:32, :] = tok
+            out_ref[d, 32:48, :] = jnp.concatenate(main[:2], axis=0).astype(bf16)
+            out_ref[d, 48:64, :] = jnp.concatenate([main[2], rest], axis=0).astype(bf16)
 
 
 def pack(ix, tok, flag, master, one, two):
@@ -52,12 +49,12 @@
     whole = lambda a: pl.BlockSpec(a.shape, lambda i, ix: (0, 0))
     return pl.pallas_call(
         pack_kernel,
-        out_shape=jax.ShapeDtypeStruct((NX * NY, 80, LANES), bf16),
+        out_shape=jax.ShapeDtypeStruct((NX * NY, 64, LANES), bf16),
         grid_spec=pltpu.PrefetchScalarGridSpec(
             num_scalar_prefetch=1,
-            grid=(NX,),
+            grid=(1,),
             in_specs=[whole(tok), whole(flag), part, part, part],
-            out_specs=pl.BlockSpec((NY, 80, LANES), lambda i, ix: (i, 0, 0)),
+            out_specs=pl.BlockSpec((NX * NY, 64, LANES), lambda i, ix: (0, 0, 0)),
         ),
         name="pack",
     )(ix, tok, flag, master, one, two)
@@ -84,7 +81,7 @@
     count = jnp.max(second_ref[:, 40:48, :].astype(f32), axis=0)
     count_ref[...] = count
     lane = lax.broadcasted_iota(jnp.int32, (8, LANES), 1)
-    mine = jnp.max(jnp.where(lane == bucket_ref[0], count, 0.0), axis=(0, 1), keepdims=True)
+    mine = jnp.max(jnp.where(lane == FLAGS + bucket_ref[0], count, 0.0), axis=(0, 1), keepdims=True)
     for x in range(NX):
         for y in range(NY):
             r = y * 32 + x * 8
@@ -92,17 +89,14 @@
                 two = first_ref[x * NY + y, 32 + 16 * k : 48 + 16 * k, :].astype(f32)
                 params[2 * k, r : r + 8, :] = two[:8]
                 params[2 * k + 1, r : r + 8, :] = two[8:]
-            params[4, r : r + 8, :] = first_ref[x * NY + y, 64:80, :].astype(f32)[:8]
     scale, fix = scale_ref[bucket_ref[0]], fix_ref[bucket_ref[0]]
     halves = []
     for lo, hi in ((0, LANES), (LANES, 160)):
         if lo == 0:
-            p = [params[k] for k in range(4)]
+            old, one, two = (params[k] for k in range(3))
         else:
-            rest = params[4]
-            p = [rest[:, 32 * k : 32 * k + 32] for k in range(4)]
-        old = p[0] + p[1]
-        new, _, _ = update(old, p[2], p[3], grad[:, lo:hi], scale, fix)
+            old, one, two = (params[3][:, 32 * k : 32 * k + 32] for k in range(3))
+        new, _, _ = update(old, one, two, grad[:, lo:hi], scale, fix)
         halves.append(jnp.where(mine == 0.0, new, old))
     weight = jnp.concatenate(halves, axis=1).T.astype(bf16)
     for x in range(NX):
@@ -122,7 +116,7 @@
         ),
         in_specs=[smem, smem, smem, vmem, vmem],
         out_specs=(vmem, vmem, vmem),
-        scratch_shapes=[pltpu.VMEM((5, NY * 32, LANES), f32)],
+        scratch_shapes=[pltpu.VMEM((4, NY * 32, LANES), f32)],
         name="block",
         compiler_params=SMALL,
     )(bucket, scale, fix, first, second)
@@ -134,11 +128,12 @@
     here = pl.ds(pl.multiple_of(i * step, LANES), step)
     result_out[...] = result_ref[...]
     pieces = []
-    for x in range(NX):
-        g = grad_ref[x, i].astype(f32)
-        tail = g[32:40]
-        pieces.append(g[:32])
-        pieces.append(jnp.concatenate([tail[:, 32 * k : 32 * k + 32] for k in range(4)], axis=0))
+    for y in range(NY // STEPS):
+        for x in range(NX):
+            g = grad_ref[x, i * (NY // STEPS) + y].astype(f32)
+            tail = g[32:40]
+            pieces.append(g[:32])
+            pieces.append(jnp.concatenate([tail[:, 32 * k : 32 * k + 32] for k in range(4)], axis=0))
     grad = jnp.concatenate(pieces, axis=1)
     commit = row_ref[0:1, here] == 0.0
     master, one, two = master_ref[:, here], one_ref[:, here], two_ref[:, here]
@@ -152,8 +147,7 @@
 
 def adam(grad, row, result, master, one, two):
     rows, width = master.shape
-    step = width // NY
-    full = pl.BlockSpec((rows, step), lambda i: (0, i))
+    full = pl.BlockSpec((rows, width // STEPS), lambda i: (0, i))
     vmem = pl.BlockSpec(memory_space=VMEM)
     return pl.pallas_call(
         adam_kernel,
@@ -162,7 +156,7 @@
             jax.ShapeDtypeStruct(master.shape, bf16),
             jax.ShapeDtypeStruct(result.shape, bf16),
         ),
-        grid=(NY,),
+        grid=(STEPS,),
         in_specs=[vmem] * 6,
         out_specs=(full, full, full, full, pl.BlockSpec(result.shape, lambda i: (0, 0))),
         name="adam",
@@ -184,8 +178,8 @@
 
     perm = [(zh * NX + x, x * NX + zh) for zh in range(NX) for x in range(NX)]
     og = lax.ppermute(out_grad.T, ("zh", "x"), perm)
-    seen = jnp.max(first[:, 72:80, :], axis=0)
-    og = jnp.concatenate([og, seen], axis=0)
+    seen = jnp.max(first[:, 56:64, :], axis=0)
+    og, scales, fixes, bucket = lax.optimization_barrier((jnp.concatenate([og, seen], axis=0), scales, fixes, bucket))
     second = exchange(jnp.broadcast_to(og[None], (NZC, *og.shape)), ZC)
 
     grad, part, count = block(bucket, scales, fixes, first, second)
@@ -193,7 +187,7 @@
     result = lax.ppermute(total.astype(bf16), ("zh", "x"), perm)
     grad = exchange(grad, XY)
 
-    counts = count[0, :BUCKETS]
+    counts = count[0, FLAGS : FLAGS + BUCKETS]
     row = jnp.stack([counts, scales, fixes, *[counts] * 5])
     row = jnp.repeat(row, bucket_width, axis=1)
     master_next, one_next, two_next, half, result = adam(grad, row, result, master, moment_one, moment_two)

time: 93.2 us -> 88 us (0.944)
  blocking collectives: 12.3 us -> 32.4 us
  waiting for transfers between devices: 41 us -> 28.4 us
  starting transfers between devices: 27.2 us -> 16.6 us
  Pallas kernels: 8.63 us -> 7.2 us
    all_to_all x1 -> x2, blocking collectives: 12.3 us -> 32.4 us  [exchange(): return lax.all_to_all(x, axes, 0, 0, tiled=True)]
    all_to_all x3 -> x2, waiting for transfers between devices: 41 us -> 28.3 us  [exchange(): return lax.all_to_all(x, axes, 0, 0, tiled=True)]
    all_to_all x3 -> x2, starting transfers between devices: 25.9 us -> 15.3 us  [exchange(): return lax.all_to_all(x, axes, 0, 0, tiled=True)]
    pallas_call x1, Pallas kernels: 3.73 us -> 2.33 us  [adam(): pl.pallas_call(adam_kernel, out_shape=(*[jax.ShapeDtypeStruct(master.shap...]
  transfers between devices with their start and end apart: 5 -> 4, of which waited for: 3 -> 2; matrix products, arithmetic and copies ran while one was open for 1% -> 1% of each run, Pallas kernels for 0% -> 0%
where the time goes in v4:
time: 88 us; the launch traced here: 87.6 us
  blocking collectives  32.4 us (37%)
  waiting for transfers between devices  28.4 us (32%)
  starting transfers between devices  16.6 us (19%)
  Pallas kernels  7.2 us (8%)
  between operations  1.4 us (2%)
  local copies, waits for them, and re-layouts  0.98 us (1%)
    all_to_all x2, blocking collectives, exchange(): return lax.all_to_all(x, axes, 0, 0, tiled=True)  32.4 us
    all_to_all x2, waiting for transfers between devices, exchange(): return lax.all_to_all(x, axes, 0, 0, tiled=True)  28.3 us
    all_to_all x2, starting transfers between devices, exchange(): return lax.all_to_all(x, axes, 0, 0, tiled=True)  15.3 us
    pallas_call x1, Pallas kernels, pack(): pl.pallas_call(pack_kernel, out_shape=jax.ShapeDtypeStruct((NX * NY, 64,...  2.84 us
    pallas_call x1, Pallas kernels, adam(): pl.pallas_call(adam_kernel, out_shape=(*[jax.ShapeDtypeStruct(master.shap...  2.33 us
    pallas_call x1, Pallas kernels, block(): pl.pallas_call(block_kernel, out_shape=(jax.ShapeDtypeStruct((NX * NY, 40...  2.03 us
  transfers between devices with their start and end apart: 4, of which 2 were waited for; matrix products, arithmetic and copies ran while one was open for 1% of the time, Pallas kernels for 0%

profile of v4, /device:TPU:8, one launch (start us, length us, event | category | flops | bytes accessed | tf_op | source)
XLA Modules:
  0.0 87.6 jit_solution(1276395781731114562)
XLA Ops:
  0.6 2.8 %pack.1 = bf16[32,64,128]{2,1,0:T(8,128)(2,1)} custom-call(s32[1]{0:T(128)} %bitcast.1.ix_ref, bf16[32,128]{1,0:T(8,128)(2,1)} %bitcast.17, s32[1,16]{1,0:T(1,128)} %flag_ref.1, f32[32,5120]{1,0:T(8,128)} %master_ref.3, f32[32,5120]{1,0:T(8,128)} %one_ref.3, f32[32,5120]{1,0:T(8,128)} %two_ref.3), custom_call_target="tpu_custom_call" | custom-call | tf_op jit(solution)/shard_map/pack/pallas_call | solution.py:50
  3.5 0.0 copy-start.4
  3.5 10.3 %all-to-all-start = ((bf16[32,64,128]{2,1,0:T(8,128)(2,1)}), bf16[32,64,128]{2,1,0:T(8,128)(2,1)S(1)}, u32[]{:S(2)}, u32[]{:S(2)}) async-start(bf16[32,64,128]{2,1,0:T(8,128)(2,1)} %pack.1), calls=%async_computation | async-start | bytes 1048576 | tf_op jit(solution)/shard_map/all_to_all | solution.py:27
  13.8 0.0 copy-done.4
  13.8 0.7 collective-permute-start
  15.1 0.0 copy-start.3
  15.1 0.6 copy-done.3
  15.8 15.6 %all-to-all-done.first_ref = bf16[32,64,128]{2,1,0:T(8,128)(2,1)S(1)} async-done(((bf16[32,64,128]{2,1,0:T(8,128)(2,1)}), bf16[32,64,128]{2,1,0:T(8,128)(2,1)S(1)}, u32[]{:S(2)}, u32[]{:S(2)}) %all-to-all-start) | async-done | bytes 524320 | tf_op jit(solution)/shard_map/all_to_all | solution.py:27
  31.4 0.0 collective-permute-done
  31.5 20.1 %all_to_all.20.second_ref = bf16[16,48,128]{2,1,0:T(8,128)(2,1)S(1)} all-to-all(bf16[16,48,128]{2,1,0:T(8,128)(2,1)S(1)} %broadcast_in_dim.17), channel_id=1, replica_groups=mesh['y'=8,'zh'=4,'zl'=2,'c'=2,'x'=4] {'zh','zl','c'}, dimensions={0} | all-to-all | bytes 393216 | tf_op jit(solution)/shard_map/all_to_all | solution.py:27
  51.6 2.0 %block.1 = (bf16[32,40,128]{2,1,0:T(8,128)(2,1)}, bf16[16,40,128]{2,1,0:T(8,128)(2,1)S(1)}, f32[8,128]{1,0:T(8,128)S(1)}) custom-call(s32[1]{0:T(128)} %bitcast.4.bucket_ref, f32[16]{0:T(128)S(1)} %get-tuple-element.19.scale_ref, f32[16]{0:T(128)S(1)} %get-tuple-element.20.fix_ref, bf16[32,64,128]{2,1,0:T(8,128)(2,1)S(1)} %all-to-all-done.first_ref, ...), custom_call_target="tpu_custom_call" | custom-call | tf_op jit(solution)/shard_map/block/pallas_call | solution.py:110
  53.6 12.3 %all_to_all.21 = bf16[16,40,128]{2,1,0:T(8,128)(2,1)S(1)} all-to-all(bf16[16,40,128]{2,1,0:T(8,128)(2,1)S(1)} %get-tuple-element.24), channel_id=1, replica_groups=mesh['y'=8,'zh'=4,'zl'=2,'c'=2,'x'=4] {'zh','zl','c'}, dimensions={0} | all-to-all | bytes 327680 | tf_op jit(solution)/shard_map/all_to_all | solution.py:27
  65.9 5.0 %all-to-all-start.2 = ((bf16[32,40,128]{2,1,0:T(8,128)(2,1)}), bf16[32,40,128]{2,1,0:T(8,128)(2,1)S(1)}, u32[]{:S(2)}, u32[]{:S(2)}) async-start(bf16[32,40,128]{2,1,0:T(8,128)(2,1)} %get-tuple-element.22), calls=%async_computation.2 | async-start | bytes 655360 | tf_op jit(solution)/shard_map/all_to_all | solution.py:27
  70.9 0.7 collective-permute-start.1
  71.6 0.6 fusion.1
  72.2 0.1 slice.7
  72.3 0.1 broadcast_in_dim.18
  72.4 0.1 reshape.24.row_ref
  72.5 0.0 collective-permute-done.1.result_ref
  72.5 12.7 %all-to-all-done.2 = bf16[32,40,128]{2,1,0:T(8,128)(2,1)S(1)} async-done(((bf16[32,40,128]{2,1,0:T(8,128)(2,1)}), bf16[32,40,128]{2,1,0:T(8,128)(2,1)S(1)}, u32[]{:S(2)}, u32[]{:S(2)}) %all-to-all-start.2) | async-done | bytes 327712 | tf_op jit(solution)/shard_map/all_to_all | solution.py:27
  85.2 0.0 copy-done.2
  85.2 0.0 copy-done
  85.2 0.0 copy-done.1
  85.2 2.3 %adam.1 = (f32[32,5120]{1,0:T(8,128)}, f32[32,5120]{1,0:T(8,128)}, f32[32,5120]{1,0:T(8,128)}, bf16[32,5120]{1,0:T(8,128)(2,1)}, bf16[40,128]{1,0:T(8,128)(2,1)}) custom-call(bf16[4,8,40,128]{3,2,1,0:T(8,128)(2,1)S(1)} %bitcast.14, f32[8,5120]{1,0:T(8,128)S(1)} %reshape.24.row_ref, bf16[40,128]{1,0:T(8,128)(2,1)S(1)} %collective-permute-done.1.result_ref, ...), custom_call_target="tpu_custom_call" | custom-call | tf_op jit(solution)/shard_map/adam/pallas_call | solution.py:152
  (9 shorter events, 0.1 us)
Async XLA Ops:
  3.5 10.3 %copy-start.4 = (bf16[128,40]{0,1:T(8,128)(2,1)S(1)}, bf16[128,40]{0,1:T(8,128)(2,1)}, u32[]{:S(2)}) copy-start(bf16[128,40]{0,1:T(8,128)(2,1)} %param.9) | copy-start | bytes 30724
  3.5 27.9 %all-to-all-start = ((bf16[32,64,128]{2,1,0:T(8,128)(2,1)}), bf16[32,64,128]{2,1,0:T(8,128)(2,1)S(1)}, u32[]{:S(2)}, u32[]{:S(2)}) async-start(bf16[32,64,128]{2,1,0:T(8,128)(2,1)} %pack.1), calls=%async_computation | async-start | bytes 1048576 | tf_op jit(solution)/shard_map/all_to_all | solution.py:27
  13.8 17.6 %collective-permute-start = (bf16[40,128]{1,0:T(8,128)(2,1)S(1)}, bf16[40,128]{1,0:T(8,128)(2,1)S(1)}, u32[]{:S(2)}, u32[]{:S(2)}) collective-permute-start(bf16[40,128]{1,0:T(8,128)(2,1)S(1)} %bitcast.18), channel_id=1, source_target_pairs={{0,0},{1,16},{2,32},{3,48},{16,1},{17,17},{18,33},{19,49},{32,2},{... | collective-permute-start | bytes 30728 | tf_op jit(solution)/shard_map/ppermute | solution.py:180
  15.1 0.7 copy-start.3
  51.6 33.6 %copy-start.2 = (f32[32,5120]{1,0:T(8,128)S(1)}, f32[32,5120]{1,0:T(8,128)}, u32[]{:S(2)}) copy-start(f32[32,5120]{1,0:T(8,128)} %two_ref.3) | copy-start | bytes 1966084
  65.9 19.4 %copy-start = (f32[32,5120]{1,0:T(8,128)S(1)}, f32[32,5120]{1,0:T(8,128)}, u32[]{:S(2)}) copy-start(f32[32,5120]{1,0:T(8,128)} %master_ref.3) | copy-start | bytes 1966084
  65.9 19.4 %copy-start.1 = (f32[32,5120]{1,0:T(8,128)S(1)}, f32[32,5120]{1,0:T(8,128)}, u32[]{:S(2)}) copy-start(f32[32,5120]{1,0:T(8,128)} %one_ref.3) | copy-start | bytes 1966084
  65.9 19.4 %all-to-all-start.2 = ((bf16[32,40,128]{2,1,0:T(8,128)(2,1)}), bf16[32,40,128]{2,1,0:T(8,128)(2,1)S(1)}, u32[]{:S(2)}, u32[]{:S(2)}) async-start(bf16[32,40,128]{2,1,0:T(8,128)(2,1)} %get-tuple-element.22), calls=%async_computation.2 | async-start | bytes 655360 | tf_op jit(solution)/shard_map/all_to_all | solution.py:27
  70.9 1.6 %collective-permute-start.1 = (bf16[40,128]{1,0:T(8,128)(2,1)S(1)}, bf16[40,128]{1,0:T(8,128)(2,1)S(1)}, u32[]{:S(2)}, u32[]{:S(2)}) collective-permute-start(bf16[40,128]{1,0:T(8,128)(2,1)S(1)} %reduce_sum.12), channel_id=1, source_target_pairs={{0,0},{1,16},{2,32},{3,48},{16,1},{17,17},{18,33},{19,49},{32,2},{... | collective-permute-start | bytes 30728 | tf_op jit(solution)/shard_map/ppermute | solution.py:187

commit v5 on v4

--- a/solution.py
+++ b/solution.py
@@ -27,37 +27,62 @@
     return lax.all_to_all(x, axes, 0, 0, tiled=True)
 
 
-def pack_kernel(ix_ref, tok_ref, flag_ref, master_ref, one_ref, two_ref, out_ref):
+def pack_kernel(tok_hbm, flag_hbm, master_hbm, one_hbm, two_hbm, out_hbm, tok_ref, flag_ref, parts_ref, out_ref, sems, sent):
+    mine = pl.ds(pl.multiple_of(lax.axis_index("x") * 8, 8), 8)
+    reads = [
+        pltpu.make_async_copy(tok_hbm, tok_ref, sems.at[0]),
+        pltpu.make_async_copy(flag_hbm, flag_ref, sems.at[1]),
+        *[
+            pltpu.make_async_copy(ref.at[mine], parts_ref.at[k], sems.at[2 + k])
+            for k, ref in enumerate((master_hbm, one_hbm, two_hbm))
+        ],
+    ]
+    for read in reads:
+        read.start()
+    reads[0].wait()
+    reads[1].wait()
+    tok = tok_ref[...]
+    for d in range(NX * NY):
+        out_ref[d, 0:32, :] = tok
     flag = jnp.concatenate([flag_ref[...].astype(f32), jnp.zeros((1, 32 - BUCKETS), f32)], axis=1)
     flag = jnp.broadcast_to(flag, (8, 32))
-    tok = tok_ref[...]
+    for read in reads[2:]:
+        read.wait()
+    writes = []
     for x in range(NX):
         for y in range(NY):
             c = (y * NX + x) * 160
             d = x * NY + y
-            parts = [p[:, c : c + 160] for p in (master_ref, one_ref, two_ref)]
+            parts = [parts_ref[k, :, c : c + 160] for k in range(3)]
             main = [p[:, :LANES] for p in parts]
             rest = jnp.concatenate([p[:, LANES:] for p in parts] + [flag], axis=1)
-            out_ref[d, 0:32, :] = tok
             out_ref[d, 32:48, :] = jnp.concatenate(main[:2], axis=0).astype(bf16)
             out_ref[d, 48:64, :] = jnp.concatenate([main[2], rest], axis=0).astype(bf16)
-
-
-def pack(ix, tok, flag, master, one, two):
-    rows = master.shape[0] // NX
-    part = pl.BlockSpec((rows, master.shape[1]), lambda i, ix: (ix[0], 0))
-    whole = lambda a: pl.BlockSpec(a.shape, lambda i, ix: (0, 0))
+        here = pl.ds(x * NY, NY)
+        writes.append(pltpu.make_async_copy(out_ref.at[here], out_hbm.at[here], sent.at[x]))
+        writes[-1].start()
+    for write in writes:
+        write.wait()
+
+
+def pack(tok, flag, master, one, two):
+    out = (NX * NY, 64, LANES)
+    anywhere = pl.BlockSpec(memory_space=pl.ANY)
     return pl.pallas_call(
         pack_kernel,
-        out_shape=jax.ShapeDtypeStruct((NX * NY, 64, LANES), bf16),
-        grid_spec=pltpu.PrefetchScalarGridSpec(
-            num_scalar_prefetch=1,
-            grid=(1,),
-            in_specs=[whole(tok), whole(flag), part, part, part],
-            out_specs=pl.BlockSpec((NX * NY, 64, LANES), lambda i, ix: (0, 0, 0)),
-        ),
+        out_shape=jax.ShapeDtypeStruct(out, bf16),
+        in_specs=[anywhere] * 5,
+        out_specs=anywhere,
+        scratch_shapes=[
+            pltpu.VMEM(tok.shape, bf16),
+            pltpu.VMEM(flag.shape, jnp.int32),
+            pltpu.VMEM((3, 8, master.shape[1]), f32),
+            pltpu.VMEM(out, bf16),
+            pltpu.SemaphoreType.DMA((5,)),
+            pltpu.SemaphoreType.DMA((NX,)),
+        ],
         name="pack",
-    )(ix, tok, flag, master, one, two)
+    )(tok, flag, master, one, two)
 
 
 def update(master, one, two, gradient, scale, fix):
@@ -66,43 +91,44 @@
     return master - scale * first / (jnp.sqrt(second * fix) + epsilon), first, second
 
 
-def block_kernel(bucket_ref, scale_ref, fix_ref, first_ref, second_ref, grad_ref, part_ref, count_ref, params):
+def block_kernel(bucket_ref, scale_ref, fix_ref, first_ref, second_ref, grad_hbm, part_ref, count_ref, message, sent):
     tok = [first_ref[x * NY : (x + 1) * NY, 0:32, :].reshape(NY * 32, LANES) for x in range(NX)]
+    tok = jnp.concatenate(tok, axis=1)
     og = [second_ref[x * NX : (x + 1) * NX, 0:40, :].reshape(160, LANES) for x in range(NX)]
-    grad = jnp.zeros((NY * 32, 160), f32)
-    for x in range(NX):
-        grad += lax.dot_general(tok[x], og[x], (((1,), (1,)), ((), ())), preferred_element_type=f32)
+    og = jnp.concatenate(og, axis=1)
+    grad = lax.dot_general(tok, og, (((1,), (1,)), ((), ())), preferred_element_type=f32)
     for y in range(NY):
         g = grad[y * 32 : (y + 1) * 32, :]
         tail = jnp.concatenate([g[8 * k : 8 * k + 8, LANES:160] for k in range(4)], axis=1)
-        g = jnp.concatenate([g[:, :LANES], tail], axis=0).astype(bf16)
-        for x in range(NX):
-            grad_ref[x * NY + y] = g
+        message[y] = jnp.concatenate([g[:, :LANES], tail], axis=0).astype(bf16)
+    writes = [pltpu.make_async_copy(message, grad_hbm.at[pl.ds(x * NY, NY)], sent.at[x]) for x in range(NX)]
+    for write in writes:
+        write.start()
     count = jnp.max(second_ref[:, 40:48, :].astype(f32), axis=0)
     count_ref[...] = count
     lane = lax.broadcasted_iota(jnp.int32, (8, LANES), 1)
     mine = jnp.max(jnp.where(lane == FLAGS + bucket_ref[0], count, 0.0), axis=(0, 1), keepdims=True)
-    for x in range(NX):
-        for y in range(NY):
-            r = y * 32 + x * 8
-            for k in range(2):
-                two = first_ref[x * NY + y, 32 + 16 * k : 48 + 16 * k, :].astype(f32)
-                params[2 * k, r : r + 8, :] = two[:8]
-                params[2 * k + 1, r : r + 8, :] = two[8:]
+    order = [x * NY + y for y in range(NY) for x in range(NX)]
+    pairs = [[first_ref[d, 32 + 16 * k : 48 + 16 * k, :].astype(f32) for d in order] for k in range(2)]
+    params = [
+        jnp.concatenate([p[8 * half : 8 * half + 8] for p in pairs[k]], axis=0) for k in range(2) for half in range(2)
+    ]
     scale, fix = scale_ref[bucket_ref[0]], fix_ref[bucket_ref[0]]
     halves = []
     for lo, hi in ((0, LANES), (LANES, 160)):
         if lo == 0:
-            old, one, two = (params[k] for k in range(3))
+            old, one, two = params[:3]
         else:
             old, one, two = (params[3][:, 32 * k : 32 * k + 32] for k in range(3))
         new, _, _ = update(old, one, two, grad[:, lo:hi], scale, fix)
         halves.append(jnp.where(mine == 0.0, new, old))
     weight = jnp.concatenate(halves, axis=1).T.astype(bf16)
+    out = jnp.dot(weight, tok, preferred_element_type=f32).astype(bf16)
     for x in range(NX):
-        out = jnp.dot(weight, tok[x], preferred_element_type=f32)
         for k in range(NX):
-            part_ref[x * NX + k] = out[40 * k : 40 * k + 40, :].astype(bf16)
+            part_ref[x * NX + k] = out[40 * k : 40 * k + 40, x * LANES : (x + 1) * LANES]
+    for write in writes:
+        write.wait()
 
 
 def block(bucket, scale, fix, first, second):
@@ -115,8 +141,8 @@
             jax.ShapeDtypeStruct((8, LANES), f32),
         ),
         in_specs=[smem, smem, smem, vmem, vmem],
-        out_specs=(vmem, vmem, vmem),
-        scratch_shapes=[pltpu.VMEM((4, NY * 32, LANES), f32)],
+        out_specs=(pl.BlockSpec(memory_space=pl.ANY), vmem, vmem),
+        scratch_shapes=[pltpu.VMEM((NY, 40, LANES), bf16), pltpu.SemaphoreType.DMA((NX,))],
         name="block",
         compiler_params=SMALL,
     )(bucket, scale, fix, first, second)
@@ -174,7 +200,7 @@
     fixes = 1.0 / (1.0 - jnp.power(f32(second_decay), times))
     bucket = ((iy * NX + ix) // 2)[None]
 
-    first = exchange(pack(ix[None], tokens.T, flags, master, moment_one, moment_two), XY)
+    first = exchange(pack(tokens.T, flags, master, moment_one, moment_two), XY)
 
     perm = [(zh * NX + x, x * NX + zh) for zh in range(NX) for x in range(NX)]
     og = lax.ppermute(out_grad.T, ("zh", "x"), perm)

time: 88 us -> 87.9 us (level)
  no operation moved by 1% of the time
where the time goes in v5:
time: 87.9 us; the launch traced here: 87.4 us
  blocking collectives  32.4 us (37%)
  waiting for transfers between devices  28.4 us (32%)
  starting transfers between devices  16.5 us (19%)
  Pallas kernels  7.1 us (8%)
  between operations  1.42 us (2%)
  local copies, waits for them, and re-layouts  0.99 us (1%)
    all_to_all x2, blocking collectives, exchange(): return lax.all_to_all(x, axes, 0, 0, tiled=True)  32.4 us
    all_to_all x2, waiting for transfers between devices, exchange(): return lax.all_to_all(x, axes, 0, 0, tiled=True)  28.3 us
    all_to_all x2, starting transfers between devices, exchange(): return lax.all_to_all(x, axes, 0, 0, tiled=True)  15.2 us
    pallas_call x1, Pallas kernels, pack(): pl.pallas_call(pack_kernel, out_shape=jax.ShapeDtypeStruct(out, bf16), in...  2.84 us
    pallas_call x1, Pallas kernels, adam(): pl.pallas_call(adam_kernel, out_shape=(*[jax.ShapeDtypeStruct(master.shap...  2.33 us
    pallas_call x1, Pallas kernels, block(): pl.pallas_call(block_kernel, out_shape=(jax.ShapeDtypeStruct((NX * NY, 40...  1.92 us
  transfers between devices with their start and end apart: 4, of which 2 were waited for; matrix products, arithmetic and copies ran while one was open for 1% of the time, Pallas kernels for 0%

profile of v5, /device:TPU:8, one launch (start us, length us, event | category | flops | bytes accessed | tf_op | source)
XLA Modules:
  0.0 87.4 jit_solution(15212004877756706494)
XLA Ops:
  0.6 2.8 %pack.1 = bf16[32,64,128]{2,1,0:T(8,128)(2,1)} custom-call(bf16[32,128]{1,0:T(8,128)(2,1)} %bitcast.16, s32[1,16]{1,0:T(1,128)} %flag_hbm.1, f32[32,5120]{1,0:T(8,128)} %master_ref.1, f32[32,5120]{1,0:T(8,128)} %one_ref.1, f32[32,5120]{1,0:T(8,128)} %two_ref.1), custom_call_target="tpu_custom_call" | custom-call | tf_op jit(solution)/shard_map/pack/pallas_call | solution.py:71
  3.5 0.0 copy-start.4
  3.5 10.2 %all-to-all-start = ((bf16[32,64,128]{2,1,0:T(8,128)(2,1)}), bf16[32,64,128]{2,1,0:T(8,128)(2,1)S(1)}, u32[]{:S(2)}, u32[]{:S(2)}) async-start(bf16[32,64,128]{2,1,0:T(8,128)(2,1)} %pack.1), calls=%async_computation | async-start | bytes 1048576 | tf_op jit(solution)/shard_map/all_to_all | solution.py:27
  13.7 0.0 copy-done.4
  13.7 0.7 collective-permute-start
  15.0 0.0 copy-start.3
  15.0 0.6 copy-done.3
  15.7 15.6 %all-to-all-done.first_ref = bf16[32,64,128]{2,1,0:T(8,128)(2,1)S(1)} async-done(((bf16[32,64,128]{2,1,0:T(8,128)(2,1)}), bf16[32,64,128]{2,1,0:T(8,128)(2,1)S(1)}, u32[]{:S(2)}, u32[]{:S(2)}) %all-to-all-start) | async-done | bytes 524320 | tf_op jit(solution)/shard_map/all_to_all | solution.py:27
  31.3 0.0 collective-permute-done
  31.4 20.1 %all_to_all.20.second_ref = bf16[16,48,128]{2,1,0:T(8,128)(2,1)S(1)} all-to-all(bf16[16,48,128]{2,1,0:T(8,128)(2,1)S(1)} %broadcast_in_dim.13), channel_id=1, replica_groups=mesh['y'=8,'zh'=4,'zl'=2,'c'=2,'x'=4] {'zh','zl','c'}, dimensions={0} | all-to-all | bytes 393216 | tf_op jit(solution)/shard_map/all_to_all | solution.py:27
  51.5 1.9 %block.1 = (bf16[32,40,128]{2,1,0:T(8,128)(2,1)}, bf16[16,40,128]{2,1,0:T(8,128)(2,1)S(1)}, f32[8,128]{1,0:T(8,128)S(1)}) custom-call(s32[1]{0:T(128)} %bitcast.3.bucket_ref, f32[16]{0:T(128)S(1)} %get-tuple-element.19.scale_ref, f32[16]{0:T(128)S(1)} %get-tuple-element.20.fix_ref, bf16[32,64,128]{2,1,0:T(8,128)(2,1)S(1)} %all-to-all-done.first_ref, ...), custom_call_target="tpu_custom_call" | custom-call | tf_op jit(solution)/shard_map/block/pallas_call | solution.py:136
  53.4 12.3 %all_to_all.21 = bf16[16,40,128]{2,1,0:T(8,128)(2,1)S(1)} all-to-all(bf16[16,40,128]{2,1,0:T(8,128)(2,1)S(1)} %get-tuple-element.24), channel_id=1, replica_groups=mesh['y'=8,'zh'=4,'zl'=2,'c'=2,'x'=4] {'zh','zl','c'}, dimensions={0} | all-to-all | bytes 327680 | tf_op jit(solution)/shard_map/all_to_all | solution.py:27
  65.7 5.0 %all-to-all-start.2 = ((bf16[32,40,128]{2,1,0:T(8,128)(2,1)}), bf16[32,40,128]{2,1,0:T(8,128)(2,1)S(1)}, u32[]{:S(2)}, u32[]{:S(2)}) async-start(bf16[32,40,128]{2,1,0:T(8,128)(2,1)} %get-tuple-element.22), calls=%async_computation.2 | async-start | bytes 655360 | tf_op jit(solution)/shard_map/all_to_all | solution.py:27
  70.7 0.7 collective-permute-start.1
  71.4 0.6 fusion.1
  72.0 0.1 slice.7
  72.1 0.1 broadcast_in_dim.14
  72.2 0.1 reshape.24.row_ref
  72.3 0.0 collective-permute-done.1.result_ref
  72.3 12.7 %all-to-all-done.2 = bf16[32,40,128]{2,1,0:T(8,128)(2,1)S(1)} async-done(((bf16[32,40,128]{2,1,0:T(8,128)(2,1)}), bf16[32,40,128]{2,1,0:T(8,128)(2,1)S(1)}, u32[]{:S(2)}, u32[]{:S(2)}) %all-to-all-start.2) | async-done | bytes 327712 | tf_op jit(solution)/shard_map/all_to_all | solution.py:27
  85.0 0.0 copy-done.2
  85.0 0.0 copy-done
  85.1 0.0 copy-done.1
  85.1 2.3 %adam.1 = (f32[32,5120]{1,0:T(8,128)}, f32[32,5120]{1,0:T(8,128)}, f32[32,5120]{1,0:T(8,128)}, bf16[32,5120]{1,0:T(8,128)(2,1)}, bf16[40,128]{1,0:T(8,128)(2,1)}) custom-call(bf16[4,8,40,128]{3,2,1,0:T(8,128)(2,1)S(1)} %bitcast.13, f32[8,5120]{1,0:T(8,128)S(1)} %reshape.24.row_ref, bf16[40,128]{1,0:T(8,128)(2,1)S(1)} %collective-permute-done.1.result_ref, ...), custom_call_target="tpu_custom_call" | custom-call | tf_op jit(solution)/shard_map/adam/pallas_call | solution.py:178
  (9 shorter events, 0.1 us)
Async XLA Ops:
  3.5 10.2 %copy-start.4 = (bf16[128,40]{0,1:T(8,128)(2,1)S(1)}, bf16[128,40]{0,1:T(8,128)(2,1)}, u32[]{:S(2)}) copy-start(bf16[128,40]{0,1:T(8,128)(2,1)} %param.9) | copy-start | bytes 30724
  3.5 27.8 %all-to-all-start = ((bf16[32,64,128]{2,1,0:T(8,128)(2,1)}), bf16[32,64,128]{2,1,0:T(8,128)(2,1)S(1)}, u32[]{:S(2)}, u32[]{:S(2)}) async-start(bf16[32,64,128]{2,1,0:T(8,128)(2,1)} %pack.1), calls=%async_computation | async-start | bytes 1048576 | tf_op jit(solution)/shard_map/all_to_all | solution.py:27
  13.7 17.6 %collective-permute-start = (bf16[40,128]{1,0:T(8,128)(2,1)S(1)}, bf16[40,128]{1,0:T(8,128)(2,1)S(1)}, u32[]{:S(2)}, u32[]{:S(2)}) collective-permute-start(bf16[40,128]{1,0:T(8,128)(2,1)S(1)} %bitcast.17), channel_id=1, source_target_pairs={{0,0},{1,16},{2,32},{3,48},{16,1},{17,17},{18,33},{19,49},{32,2},{... | collective-permute-start | bytes 30728 | tf_op jit(solution)/shard_map/ppermute | solution.py:206
  15.0 0.7 copy-start.3
  51.5 33.6 %copy-start.2 = (f32[32,5120]{1,0:T(8,128)S(1)}, f32[32,5120]{1,0:T(8,128)}, u32[]{:S(2)}) copy-start(f32[32,5120]{1,0:T(8,128)} %two_ref.1) | copy-start | bytes 1966084
  65.7 19.4 %copy-start = (f32[32,5120]{1,0:T(8,128)S(1)}, f32[32,5120]{1,0:T(8,128)}, u32[]{:S(2)}) copy-start(f32[32,5120]{1,0:T(8,128)} %master_ref.1) | copy-start | bytes 1966084
  65.7 19.4 %copy-start.1 = (f32[32,5120]{1,0:T(8,128)S(1)}, f32[32,5120]{1,0:T(8,128)}, u32[]{:S(2)}) copy-start(f32[32,5120]{1,0:T(8,128)} %one_ref.1) | copy-start | bytes 1966084
  65.7 19.4 %all-to-all-start.2 = ((bf16[32,40,128]{2,1,0:T(8,128)(2,1)}), bf16[32,40,128]{2,1,0:T(8,128)(2,1)S(1)}, u32[]{:S(2)}, u32[]{:S(2)}) async-start(bf16[32,40,128]{2,1,0:T(8,128)(2,1)} %get-tuple-element.22), calls=%async_computation.2 | async-start | bytes 655360 | tf_op jit(solution)/shard_map/all_to_all | solution.py:27
  70.7 1.6 %collective-permute-start.1 = (bf16[40,128]{1,0:T(8,128)(2,1)S(1)}, bf16[40,128]{1,0:T(8,128)(2,1)S(1)}, u32[]{:S(2)}, u32[]{:S(2)}) collective-permute-start(bf16[40,128]{1,0:T(8,128)(2,1)S(1)} %reduce_sum.12), channel_id=1, source_target_pairs={{0,0},{1,16},{2,32},{3,48},{16,1},{17,17},{18,33},{19,49},{32,2},{... | collective-permute-start | bytes 30728 | tf_op jit(solution)/shard_map/ppermute | solution.py:213

commit v6 on v5

--- a/solution.py
+++ b/solution.py
@@ -12,7 +12,7 @@
 ZC = ("zh", "zl", "c")
 XY = ("x", "y")
 NX, NY, NZC = 4, 8, 16
-STEPS = 4
+STEPS = 2
 LANES = 128
 FLAGS = 96
 first_decay = 0.9
@@ -91,7 +91,7 @@
     return master - scale * first / (jnp.sqrt(second * fix) + epsilon), first, second
 
 
-def block_kernel(bucket_ref, scale_ref, fix_ref, first_ref, second_ref, grad_hbm, part_ref, count_ref, message, sent):
+def block_kernel(row_ref, first_ref, second_ref, grad_hbm, part_ref, count_ref, message, sent):
     tok = [first_ref[x * NY : (x + 1) * NY, 0:32, :].reshape(NY * 32, LANES) for x in range(NX)]
     tok = jnp.concatenate(tok, axis=1)
     og = [second_ref[x * NX : (x + 1) * NX, 0:40, :].reshape(160, LANES) for x in range(NX)]
@@ -107,13 +107,14 @@
     count = jnp.max(second_ref[:, 40:48, :].astype(f32), axis=0)
     count_ref[...] = count
     lane = lax.broadcasted_iota(jnp.int32, (8, LANES), 1)
-    mine = jnp.max(jnp.where(lane == FLAGS + bucket_ref[0], count, 0.0), axis=(0, 1), keepdims=True)
+    bucket = FLAGS + lax.div(lax.axis_index("y") * NX + lax.axis_index("x"), 2)
+    pick = lambda v: jnp.max(jnp.where(lane == bucket, v, 0.0), axis=(0, 1), keepdims=True)
+    mine, scale, fix = pick(count), pick(jnp.broadcast_to(row_ref[0:1, :], (8, LANES))), pick(jnp.broadcast_to(row_ref[1:2, :], (8, LANES)))
     order = [x * NY + y for y in range(NY) for x in range(NX)]
     pairs = [[first_ref[d, 32 + 16 * k : 48 + 16 * k, :].astype(f32) for d in order] for k in range(2)]
     params = [
         jnp.concatenate([p[8 * half : 8 * half + 8] for p in pairs[k]], axis=0) for k in range(2) for half in range(2)
     ]
-    scale, fix = scale_ref[bucket_ref[0]], fix_ref[bucket_ref[0]]
     halves = []
     for lo, hi in ((0, LANES), (LANES, 160)):
         if lo == 0:
@@ -131,8 +132,8 @@
         write.wait()
 
 
-def block(bucket, scale, fix, first, second):
-    smem, vmem = pl.BlockSpec(memory_space=SMEM), pl.BlockSpec(memory_space=VMEM)
+def block(row, first, second):
+    vmem = pl.BlockSpec(memory_space=VMEM)
     return pl.pallas_call(
         block_kernel,
         out_shape=(
@@ -140,12 +141,12 @@
             jax.ShapeDtypeStruct((NZC, 40, LANES), bf16),
             jax.ShapeDtypeStruct((8, LANES), f32),
         ),
-        in_specs=[smem, smem, smem, vmem, vmem],
+        in_specs=[vmem, vmem, vmem],
         out_specs=(pl.BlockSpec(memory_space=pl.ANY), vmem, vmem),
         scratch_shapes=[pltpu.VMEM((NY, 40, LANES), bf16), pltpu.SemaphoreType.DMA((NX,))],
         name="block",
         compiler_params=SMALL,
-    )(bucket, scale, fix, first, second)
+    )(row, first, second)
 
 
 def adam_kernel(grad_ref, row_ref, result_ref, master_ref, one_ref, two_ref, master_out, one_out, two_out, half_out, result_out):
@@ -193,22 +194,21 @@
 def local(tokens, out_grad, master, moment_one, moment_two, flags, steps, rate):
     rows, width = master.shape
     bucket_width = width // BUCKETS
-    ix, iy = lax.axis_index("x"), lax.axis_index("y")
 
     times = (steps + 1).astype(f32)
     scales = rate[0] / (1.0 - jnp.power(f32(first_decay), times))
     fixes = 1.0 / (1.0 - jnp.power(f32(second_decay), times))
-    bucket = ((iy * NX + ix) // 2)[None]
+    own = jnp.pad(jnp.stack([scales, fixes]), ((0, 6), (FLAGS, LANES - FLAGS - BUCKETS)))
 
     first = exchange(pack(tokens.T, flags, master, moment_one, moment_two), XY)
 
     perm = [(zh * NX + x, x * NX + zh) for zh in range(NX) for x in range(NX)]
     og = lax.ppermute(out_grad.T, ("zh", "x"), perm)
     seen = jnp.max(first[:, 56:64, :], axis=0)
-    og, scales, fixes, bucket = lax.optimization_barrier((jnp.concatenate([og, seen], axis=0), scales, fixes, bucket))
+    og, scales, fixes, own = lax.optimization_barrier((jnp.concatenate([og, seen], axis=0), scales, fixes, own))
     second = exchange(jnp.broadcast_to(og[None], (NZC, *og.shape)), ZC)
 
-    grad, part, count = block(bucket, scales, fixes, first, second)
+    grad, part, count = block(own, first, second)
     total = jnp.sum(exchange(part, ZC).astype(f32), axis=0)
     result = lax.ppermute(total.astype(bf16), ("zh", "x"), perm)
     grad = exchange(grad, XY)

time: 87.9 us -> 86.8 us (0.987)
  Pallas kernels: 7.1 us -> 6.01 us
where the time goes in v6:
time: 86.8 us; the launch traced here: 86.3 us
  blocking collectives  32.4 us (37%)
  waiting for transfers between devices  28.3 us (33%)
  starting transfers between devices  16.5 us (19%)
  Pallas kernels  6.01 us (7%)
  between operations  1.4 us (2%)
  local copies, waits for them, and re-layouts  0.99 us (1%)
    all_to_all x2, blocking collectives, exchange(): return lax.all_to_all(x, axes, 0, 0, tiled=True)  32.4 us
    all_to_all x2, waiting for transfers between devices, exchange(): return lax.all_to_all(x, axes, 0, 0, tiled=True)  28.3 us
    all_to_all x2, starting transfers between devices, exchange(): return lax.all_to_all(x, axes, 0, 0, tiled=True)  15.2 us
    pallas_call x1, Pallas kernels, pack(): pl.pallas_call(pack_kernel, out_shape=jax.ShapeDtypeStruct(out, bf16), in...  2.84 us
    pallas_call x1, Pallas kernels, adam(): pl.pallas_call(adam_kernel, out_shape=(*[jax.ShapeDtypeStruct(master.shap...  1.77 us
  transfers between devices with their start and end apart: 4, of which 2 were waited for; matrix products, arithmetic and copies ran while one was open for 1% of the time, Pallas kernels for 0%

profile of v6, /device:TPU:8, one launch (start us, length us, event | category | flops | bytes accessed | tf_op | source)
XLA Modules:
  0.0 86.3 jit_solution(17354080481565189326)
XLA Ops:
  0.6 2.8 %pack.1 = bf16[32,64,128]{2,1,0:T(8,128)(2,1)} custom-call(bf16[32,128]{1,0:T(8,128)(2,1)} %bitcast.15, s32[1,16]{1,0:T(1,128)} %flag_hbm.1, f32[32,5120]{1,0:T(8,128)} %master_ref.1, f32[32,5120]{1,0:T(8,128)} %one_ref.1, f32[32,5120]{1,0:T(8,128)} %two_ref.1), custom_call_target="tpu_custom_call" | custom-call | tf_op jit(solution)/shard_map/pack/pallas_call | solution.py:71
  3.5 0.0 copy-start.4
  3.5 10.2 %all-to-all-start = ((bf16[32,64,128]{2,1,0:T(8,128)(2,1)}), bf16[32,64,128]{2,1,0:T(8,128)(2,1)S(1)}, u32[]{:S(2)}, u32[]{:S(2)}) async-start(bf16[32,64,128]{2,1,0:T(8,128)(2,1)} %pack.1), calls=%async_computation | async-start | bytes 1048576 | tf_op jit(solution)/shard_map/all_to_all | solution.py:27
  13.7 0.0 copy-done.4
  13.7 0.7 collective-permute-start
  15.0 0.0 copy-start.3
  15.0 0.6 copy-done.3
  15.7 0.1 select_maximum_fusion.row_ref
  15.8 15.5 %all-to-all-done.first_ref = bf16[32,64,128]{2,1,0:T(8,128)(2,1)S(1)} async-done(((bf16[32,64,128]{2,1,0:T(8,128)(2,1)}), bf16[32,64,128]{2,1,0:T(8,128)(2,1)S(1)}, u32[]{:S(2)}, u32[]{:S(2)}) %all-to-all-start) | async-done | bytes 524320 | tf_op jit(solution)/shard_map/all_to_all | solution.py:27
  31.3 0.0 collective-permute-done
  31.4 20.1 %all_to_all.20.second_ref = bf16[16,48,128]{2,1,0:T(8,128)(2,1)S(1)} all-to-all(bf16[16,48,128]{2,1,0:T(8,128)(2,1)S(1)} %broadcast_in_dim.4), channel_id=1, replica_groups=mesh['y'=8,'zh'=4,'zl'=2,'c'=2,'x'=4] {'zh','zl','c'}, dimensions={0} | all-to-all | bytes 393216 | tf_op jit(solution)/shard_map/all_to_all | solution.py:27
  51.5 1.4 %block.1 = (bf16[32,40,128]{2,1,0:T(8,128)(2,1)}, bf16[16,40,128]{2,1,0:T(8,128)(2,1)S(1)}, f32[8,128]{1,0:T(8,128)S(1)}) custom-call(f32[8,128]{1,0:T(8,128)S(1)} %select_maximum_fusion.row_ref, bf16[32,64,128]{2,1,0:T(8,128)(2,1)S(1)} %all-to-all-done.first_ref, bf16[16,48,128]{2,1,0:T(8,128)(2,1)S(1)} %all_to_all.20.second_ref), custom_call_target="tpu_custom_call" | custom-call | tf_op jit(solution)/shard_map/block/pallas_call | solution.py:137
  52.9 12.3 %all_to_all.21 = bf16[16,40,128]{2,1,0:T(8,128)(2,1)S(1)} all-to-all(bf16[16,40,128]{2,1,0:T(8,128)(2,1)S(1)} %get-tuple-element.24), channel_id=1, replica_groups=mesh['y'=8,'zh'=4,'zl'=2,'c'=2,'x'=4] {'zh','zl','c'}, dimensions={0} | all-to-all | bytes 327680 | tf_op jit(solution)/shard_map/all_to_all | solution.py:27
  65.2 5.0 %all-to-all-start.2 = ((bf16[32,40,128]{2,1,0:T(8,128)(2,1)}), bf16[32,40,128]{2,1,0:T(8,128)(2,1)S(1)}, u32[]{:S(2)}, u32[]{:S(2)}) async-start(bf16[32,40,128]{2,1,0:T(8,128)(2,1)} %get-tuple-element.20), calls=%async_computation.2 | async-start | bytes 655360 | tf_op jit(solution)/shard_map/all_to_all | solution.py:27
  70.2 0.7 collective-permute-start.1
  70.9 0.6 fusion.3
  71.5 0.1 slice.7
  71.6 0.1 broadcast_in_dim.10
  71.7 0.1 reshape.24.row_ref
  71.8 0.0 collective-permute-done.1.result_ref
  71.8 12.7 %all-to-all-done.2 = bf16[32,40,128]{2,1,0:T(8,128)(2,1)S(1)} async-done(((bf16[32,40,128]{2,1,0:T(8,128)(2,1)}), bf16[32,40,128]{2,1,0:T(8,128)(2,1)S(1)}, u32[]{:S(2)}, u32[]{:S(2)}) %all-to-all-start.2) | async-done | bytes 327712 | tf_op jit(solution)/shard_map/all_to_all | solution.py:27
  84.5 0.0 copy-done.2
  84.5 0.0 copy-done
  84.5 1.8 %adam.1 = (f32[32,5120]{1,0:T(8,128)}, f32[32,5120]{1,0:T(8,128)}, f32[32,5120]{1,0:T(8,128)}, bf16[32,5120]{1,0:T(8,128)(2,1)}, bf16[40,128]{1,0:T(8,128)(2,1)}) custom-call(bf16[4,8,40,128]{3,2,1,0:T(8,128)(2,1)S(1)} %bitcast.14, f32[8,5120]{1,0:T(8,128)S(1)} %reshape.24.row_ref, bf16[40,128]{1,0:T(8,128)(2,1)S(1)} %collective-permute-done.1.result_ref, ...), custom_call_target="tpu_custom_call" | custom-call | tf_op jit(solution)/shard_map/adam/pallas_call | solution.py:179
  (10 shorter events, 0.1 us)
Async XLA Ops:
  3.5 10.2 %copy-start.4 = (bf16[128,40]{0,1:T(8,128)(2,1)S(1)}, bf16[128,40]{0,1:T(8,128)(2,1)}, u32[]{:S(2)}) copy-start(bf16[128,40]{0,1:T(8,128)(2,1)} %param.9) | copy-start | bytes 30724
  3.5 27.8 %all-to-all-start = ((bf16[32,64,128]{2,1,0:T(8,128)(2,1)}), bf16[32,64,128]{2,1,0:T(8,128)(2,1)S(1)}, u32[]{:S(2)}, u32[]{:S(2)}) async-start(bf16[32,64,128]{2,1,0:T(8,128)(2,1)} %pack.1), calls=%async_computation | async-start | bytes 1048576 | tf_op jit(solution)/shard_map/all_to_all | solution.py:27
  13.7 17.6 %collective-permute-start = (bf16[40,128]{1,0:T(8,128)(2,1)S(1)}, bf16[40,128]{1,0:T(8,128)(2,1)S(1)}, u32[]{:S(2)}, u32[]{:S(2)}) collective-permute-start(bf16[40,128]{1,0:T(8,128)(2,1)S(1)} %bitcast.20), channel_id=1, source_target_pairs={{0,0},{1,16},{2,32},{3,48},{16,1},{17,17},{18,33},{19,49},{32,2},{... | collective-permute-start | bytes 30728 | tf_op jit(solution)/shard_map/ppermute | solution.py:206
  15.0 0.7 copy-start.3
  51.5 33.0 %copy-start.2 = (f32[32,5120]{1,0:T(8,128)S(1)}, f32[32,5120]{1,0:T(8,128)}, u32[]{:S(2)}) copy-start(f32[32,5120]{1,0:T(8,128)} %two_ref.1) | copy-start | bytes 1966084
  65.2 19.4 %copy-start = (f32[32,5120]{1,0:T(8,128)S(1)}, f32[32,5120]{1,0:T(8,128)}, u32[]{:S(2)}) copy-start(f32[32,5120]{1,0:T(8,128)} %master_ref.1) | copy-start | bytes 1966084
  65.2 19.4 %copy-start.1 = (f32[32,5120]{1,0:T(8,128)S(1)}, f32[32,5120]{1,0:T(8,128)}, u32[]{:S(2)}) copy-start(f32[32,5120]{1,0:T(8,128)} %one_ref.1) | copy-start | bytes 1966084
  65.2 19.4 %all-to-all-start.2 = ((bf16[32,40,128]{2,1,0:T(8,128)(2,1)}), bf16[32,40,128]{2,1,0:T(8,128)(2,1)S(1)}, u32[]{:S(2)}, u32[]{:S(2)}) async-start(bf16[32,40,128]{2,1,0:T(8,128)(2,1)} %get-tuple-element.20), calls=%async_computation.2 | async-start | bytes 655360 | tf_op jit(solution)/shard_map/all_to_all | solution.py:27
  70.2 1.6 %collective-permute-start.1 = (bf16[40,128]{1,0:T(8,128)(2,1)S(1)}, bf16[40,128]{1,0:T(8,128)(2,1)S(1)}, u32[]{:S(2)}, u32[]{:S(2)}) collective-permute-start(bf16[40,128]{1,0:T(8,128)(2,1)S(1)} %reduce_sum.12), channel_id=1, source_target_pairs={{0,0},{1,16},{2,32},{3,48},{16,1},{17,17},{18,33},{19,49},{32,2},{... | collective-permute-start | bytes 30728 | tf_op jit(solution)/shard_map/ppermute | solution.py:213

commit v7 on v6

v7 whole, which is shorter than its diff:
```python
import jax
import jax.numpy as jnp
from jax import lax
from jax.experimental import pallas as pl
from jax.experimental.pallas import tpu as pltpu
from jax.sharding import Mesh
from jax.sharding import PartitionSpec as P

BUCKETS = 16
FSDP = ("yq", "yp", "zq", "zp", "c")
ALL = FSDP + ("x",)
NEAR = ("x", "yp", "zp", "c")
FAR = ("yq", "zq")
NX, NE, NFAR = 4, 8, 16
STEPS = 2
LANES = 128
FLAGS = 96
first_decay = 0.9
second_decay = 0.95
epsilon = 1e-08
bf16, f32 = jnp.bfloat16, jnp.float32
VMEM = pltpu.VMEM
SMALL = pltpu.CompilerParams(vmem_limit_bytes=16 * 1024 * 1024)


def runs(x, e):
    yp, zc = e // 4, e % 4
    return [(2 * x + yp) * 640 + 160 * k + 40 * zc for k in range(4)]


def exchange(x, axes):
    return lax.all_to_all(x, axes, 0, 0, tiled=True)


def pack_kernel(tok_hbm, flag_hbm, master_hbm, one_hbm, two_hbm, out_hbm, tok_ref, flag_ref, parts_ref, out_ref, sems, sent):
    mine = pl.ds(pl.multiple_of(lax.axis_index("x") * 8, 8), 8)
    reads = [
        pltpu.make_async_copy(tok_hbm, tok_ref, sems.at[0]),
        pltpu.make_async_copy(flag_hbm, flag_ref, sems.at[1]),
        *[
            pltpu.make_async_copy(ref.at[mine], parts_ref.at[k], sems.at[2 + k])
            for k, ref in enumerate((master_hbm, one_hbm, two_hbm))
        ],
    ]
    for read in reads:
        read.start()
    reads[0].wait()
    reads[1].wait()
    tok = tok_ref[...]
    for d in range(NX * NE):
        out_ref[d, 0:32, :] = tok
    flag = jnp.concatenate([flag_ref[...].astype(f32), jnp.zeros((1, 32 - BUCKETS), f32)], axis=1)
    flag = jnp.broadcast_to(flag, (8, 32))
    for read in reads[2:]:
        read.wait()
    writes = []
    for x in range(NX):
        for e in range(NE):
            d = x * NE + e
            parts = [
                jnp.concatenate([parts_ref[k, :, c : c + 40] for c in runs(x, e)], axis=1) for k in range(3)
            ]
            main = [p[:, :LANES] for p in parts]
            rest = jnp.concatenate([p[:, LANES:] for p in parts] + [flag], axis=1)
            out_ref[d, 32:48, :] = jnp.concatenate(main[:2], axis=0).astype(bf16)
            out_ref[d, 48:64, :] = jnp.concatenate([main[2], rest], axis=0).astype(bf16)
        here = pl.ds(x * NE, NE)
        writes.append(pltpu.make_async_copy(out_ref.at[here], out_hbm.at[here], sent.at[x]))
        writes[-1].start()
    for write in writes:
        write.wait()


def pack(tok, flag, master, one, two):
    out = (NX * NE, 64, LANES)
    anywhere = pl.BlockSpec(memory_space=pl.ANY)
    return pl.pallas_call(
        pack_kernel,
        out_shape=jax.ShapeDtypeStruct(out, bf16),
        in_specs=[anywhere] * 5,
        out_specs=anywhere,
        scratch_shapes=[
            pltpu.VMEM(tok.shape, bf16),
            pltpu.VMEM(flag.shape, jnp.int32),
            pltpu.VMEM((3, 8, master.shape[1]), f32),
            pltpu.VMEM(out, bf16),
            pltpu.SemaphoreType.DMA((5,)),
            pltpu.SemaphoreType.DMA((NX,)),
        ],
        name="pack",
    )(tok, flag, master, one, two)


def update(master, one, two, gradient, scale, fix):
    first = first_decay * one + (1.0 - first_decay) * gradient
    second = second_decay * two + (1.0 - second_decay) * gradient * gradient
    return master - scale * first / (jnp.sqrt(second * fix) + epsilon), first, second


def block_kernel(row_ref, first_ref, second_ref, grad_hbm, part_ref, count_ref, message, sent):
    tok = [first_ref[x * NE : (x + 1) * NE, 0:32, :].reshape(NE * 32, LANES) for x in range(NX)]
    tok = jnp.concatenate(tok, axis=1)
    og = [second_ref[x * NX : (x + 1) * NX, 0:40, :].reshape(160, LANES) for x in range(NX)]
    og = jnp.concatenate(og, axis=1)
    grad = lax.dot_general(tok, og, (((1,), (1,)), ((), ())), preferred_element_type=f32)
    for y in range(NE):
        g = grad[y * 32 : (y + 1) * 32, :]
        tail = jnp.concatenate([g[8 * k : 8 * k + 8, LANES:160] for k in range(4)], axis=1)
        message[y] = jnp.concatenate([g[:, :LANES], tail], axis=0).astype(bf16)
    writes = [pltpu.make_async_copy(message, grad_hbm.at[pl.ds(x * NE, NE)], sent.at[x]) for x in range(NX)]
    for write in writes:
        write.start()
    count = jnp.max(second_ref[:, 40:48, :].astype(f32), axis=0)
    count_ref[...] = count
    lane = lax.broadcasted_iota(jnp.int32, (8, LANES), 1)
    bucket = FLAGS + 4 * lax.axis_index("x") + 2 * lax.axis_index("yp")
    table = [count, *[jnp.broadcast_to(row_ref[k : k + 1, :], (8, LANES)) for k in range(2)]]
    pick = lambda v, b: jnp.max(jnp.where(lane == b, v, 0.0), axis=(0, 1), keepdims=True)
    both = [[pick(v, bucket + k) for k in range(2)] for v in table]
    order = [x * NE + y for y in range(NE) for x in range(NX)]
    pairs = [[first_ref[d, 32 + 16 * k : 48 + 16 * k, :].astype(f32) for d in order] for k in range(2)]
    params = [
        jnp.concatenate([p[8 * half : 8 * half + 8] for p in pairs[k]], axis=0) for k in range(2) for half in range(2)
    ]
    halves = []
    for lo, hi in ((0, LANES), (LANES, 160)):
        if lo == 0:
            old, one, two = params[:3]
        else:
            old, one, two = (params[3][:, 32 * k : 32 * k + 32] for k in range(3))
        early = lax.broadcasted_iota(jnp.int32, (1, hi - lo), 1) + lo < 80
        mine, scale, fix = (jnp.where(early, *v) for v in both)
        new, _, _ = update(old, one, two, grad[:, lo:hi], scale, fix)
        halves.append(jnp.where(mine == 0.0, new, old))
    weight = jnp.concatenate(halves, axis=1).T.astype(bf16)
    out = jnp.dot(weight, tok, preferred_element_type=f32).astype(bf16)
    for x in range(NX):
        for k in range(NX):
            part_ref[x * NX + k] = out[40 * k : 40 * k + 40, x * LANES : (x + 1) * LANES]
    for write in writes:
        write.wait()


def block(row, first, second):
    vmem = pl.BlockSpec(memory_space=VMEM)
    return pl.pallas_call(
        block_kernel,
        out_shape=(
            jax.ShapeDtypeStruct((NX * NE, 40, LANES), bf16),
            jax.ShapeDtypeStruct((NFAR, 40, LANES), bf16),
            jax.ShapeDtypeStruct((8, LANES), f32),
        ),
        in_specs=[vmem, vmem, vmem],
        out_specs=(pl.BlockSpec(memory_space=pl.ANY), vmem, vmem),
        scratch_shapes=[pltpu.VMEM((NE, 40, LANES), bf16), pltpu.SemaphoreType.DMA((NX,))],
        name="block",
        compiler_params=SMALL,
    )(row, first, second)


def adam_kernel(grad_ref, row_ref, master_ref, one_ref, two_ref, master_out, one_out, two_out, half_out):
    step = master_out.shape[1]
    i = pl.program_id(0)
    here = pl.ds(pl.multiple_of(i * step, LANES), step)
    pieces = []
    for y in range(NE // STEPS):
        block = i * (NE // STEPS) + y
        got = []
        for zc in range(4):
            g = grad_ref[block * 4 + zc].astype(f32)
            tail = g[32:40]
            tail = jnp.concatenate([tail[:, 32 * k : 32 * k + 32] for k in range(4)], axis=0)
            got.append(jnp.concatenate([g[:32], tail], axis=1))
        pieces += [got[zc][:, 40 * k : 40 * k + 40] for k in range(4) for zc in range(4)]
    grad = jnp.concatenate(pieces, axis=1)
    commit = row_ref[0:1, here] == 0.0
    master, one, two = master_ref[:, here], one_ref[:, here], two_ref[:, here]
    new, first, second = update(master, one, two, grad, row_ref[1:2, here], row_ref[2:3, here])
    master = jnp.where(commit, new, master)
    master_out[...] = master
    half_out[...] = master.astype(bf16)
    one_out[...] = jnp.where(commit, first, one)
    two_out[...] = jnp.where(commit, second, two)


def adam(grad, row, master, one, two):
    rows, width = master.shape
    full = pl.BlockSpec((rows, width // STEPS), lambda i: (0, i))
    vmem = pl.BlockSpec(memory_space=VMEM)
    return pl.pallas_call(
        adam_kernel,
        out_shape=(
            *[jax.ShapeDtypeStruct(master.shape, f32)] * 3,
            jax.ShapeDtypeStruct(master.shape, bf16),
        ),
        grid=(STEPS,),
        in_specs=[vmem] * 5,
        out_specs=(full, full, full, full),
        name="adam",
        compiler_params=SMALL,
    )(grad, row, master, one, two)


def local(tokens, out_grad, master, moment_one, moment_two, flags, steps, rate):
    _, width = master.shape
    bucket_width = width // BUCKETS

    times = (steps + 1).astype(f32)
    scales = rate[0] / (1.0 - jnp.power(f32(first_decay), times))
    fixes = 1.0 / (1.0 - jnp.power(f32(second_decay), times))
    own = jnp.pad(jnp.stack([scales, fixes]), ((0, 6), (FLAGS, LANES - FLAGS - BUCKETS)))

    first = exchange(pack(tokens.T, flags, master, moment_one, moment_two), NEAR)

    perm = [(yq * NX + x, x * NX + yq) for yq in range(NX) for x in range(NX)]
    og = lax.ppermute(out_grad.T, ("yq", "x"), perm)
    seen = jnp.max(first[:, 56:64, :], axis=0)
    og, scales, fixes, own = lax.optimization_barrier((jnp.concatenate([og, seen], axis=0), scales, fixes, own))
    second = exchange(jnp.broadcast_to(og[None], (NFAR, *og.shape)), FAR)

    grad, part, count = block(own, first, second)
    total = jnp.sum(exchange(part, FAR).astype(f32), axis=0)
    result = lax.ppermute(total.astype(bf16), ("yq", "x"), perm)
    grad = exchange(grad, NEAR)

    counts = count[0, FLAGS : FLAGS + BUCKETS]
    row = jnp.stack([counts, scales, fixes, *[counts] * 5])
    row = jnp.repeat(row, bucket_width, axis=1)
    master_next, one_next, two_next, half = adam(grad, row, master, moment_one, moment_two)
    steps_next = steps + (counts == 0).astype(jnp.int32)
    return master_next, one_next, two_next, half, steps_next, result.T


def solution(mesh):
    split = Mesh(mesh.devices.reshape(4, 2, 4, 2, 2, 4), ALL)
    in_specs = (P("x", FSDP), P("x", FSDP), P(FSDP), P(FSDP), P(FSDP), P(ALL), P(), P())
    out_specs = (P(FSDP), P(FSDP), P(FSDP), P(FSDP), P(), P("x", FSDP))
    return jax.shard_map(local, mesh=split, in_specs=in_specs, out_specs=out_specs, check_vma=False)
```

time: 86.8 us -> 87.7 us (1.010)
  the two profiles are of different devices: /device:TPU:8 before, /device:TPU:4 now
where the time goes in v7:
time: 87.7 us; the launch traced here: 87.1 us
  blocking collectives  38.9 us (44%)
  starting transfers between devices  24.4 us (28%)
  waiting for transfers between devices  13.2 us (15%)
  Pallas kernels  6.87 us (8%)
  local copies, waits for them, and re-layouts  1.59 us (2%)
  between operations  1.39 us (2%)
    all_to_all x2, blocking collectives, exchange(): return lax.all_to_all(x, axes, 0, 0, tiled=True)  38.9 us
    all_to_all x2, starting transfers between devices, exchange(): return lax.all_to_all(x, axes, 0, 0, tiled=True)  16.2 us
    ppermute x1, waiting for transfers between devices, local(): result = lax.ppermute(total.astype(bf16), ('yq', 'x'), perm)  7.52 us
    ppermute x1, starting transfers between devices, local(): og = lax.ppermute(out_grad.T, ('yq', 'x'), perm)  4.79 us
    pallas_call x1, Pallas kernels, pack(): pl.pallas_call(pack_kernel, out_shape=jax.ShapeDtypeStruct(out, bf16), in...  3.56 us
    ppermute x1, starting transfers between devices, local(): result = lax.ppermute(total.astype(bf16), ('yq', 'x'), perm)  3.47 us
    all_to_all x2, waiting for transfers between devices, exchange(): return lax.all_to_all(x, axes, 0, 0, tiled=True)  2.86 us
    ppermute x1, waiting for transfers between devices, local(): og = lax.ppermute(out_grad.T, ('yq', 'x'), perm)  2.79 us
  transfers between devices with their start and end apart: 4, of which 3 were waited for; matrix products, arithmetic and copies ran while one was open for 1% of the time, Pallas kernels for 0%

profile of v7, /device:TPU:4, one launch (start us, length us, event | category | flops | bytes accessed | tf_op | source)
XLA Modules:
  0.0 87.1 jit_solution(1147434725585796673)
XLA Ops:
  0.6 3.6 %pack.1 = bf16[32,64,128]{2,1,0:T(8,128)(2,1)} custom-call(bf16[32,128]{1,0:T(8,128)(2,1)} %bitcast.14, s32[1,16]{1,0:T(1,128)} %flag_hbm.1, f32[32,5120]{1,0:T(8,128)} %master_ref.1, f32[32,5120]{1,0:T(8,128)} %one_ref.1, f32[32,5120]{1,0:T(8,128)} %two_ref.1), custom_call_target="tpu_custom_call" | custom-call | tf_op jit(solution)/shard_map/pack/pallas_call | solution.py:77
  4.2 0.0 copy-start.4
  4.2 9.5 %all-to-all-start = ((bf16[32,64,128]{2,1,0:T(8,128)(2,1)}), bf16[32,64,128]{2,1,0:T(8,128)(2,1)S(1)}, u32[]{:S(2)}, u32[]{:S(2)}) async-start(bf16[32,64,128]{2,1,0:T(8,128)(2,1)} %pack.1), calls=%async_computation | async-start | bytes 1048576 | tf_op jit(solution)/shard_map/all_to_all | solution.py:32
  13.7 0.0 copy-done.4
  13.7 4.8 %collective-permute-start = (bf16[40,128]{1,0:T(8,128)(2,1)S(1)}, bf16[40,128]{1,0:T(8,128)(2,1)S(1)}, u32[]{:S(2)}, u32[]{:S(2)}) collective-permute-start(bf16[40,128]{1,0:T(8,128)(2,1)S(1)} %bitcast.19), channel_id=1, source_target_pairs={{0,0},{1,128},{2,256},{3,384},{128,1},{129,129},{130,257},{131,385... | collective-permute-start | bytes 30728 | tf_op jit(solution)/shard_map/ppermute | solution.py:216
  19.2 0.0 copy-start.3
  19.2 0.6 copy-done.3
  19.9 0.1 select_maximum_fusion.row_ref
  19.9 2.9 %all-to-all-done.first_ref = bf16[32,64,128]{2,1,0:T(8,128)(2,1)S(1)} async-done(((bf16[32,64,128]{2,1,0:T(8,128)(2,1)}), bf16[32,64,128]{2,1,0:T(8,128)(2,1)S(1)}, u32[]{:S(2)}, u32[]{:S(2)}) %all-to-all-start) | async-done | bytes 524320 | tf_op jit(solution)/shard_map/all_to_all | solution.py:32
  22.8 2.8 %collective-permute-done = bf16[40,128]{1,0:T(8,128)(2,1)S(1)} collective-permute-done((bf16[40,128]{1,0:T(8,128)(2,1)S(1)}, bf16[40,128]{1,0:T(8,128)(2,1)S(1)}, u32[]{:S(2)}, u32[]{:S(2)}) %collective-permute-start) | collective-permute-done | bytes 10272 | tf_op jit(solution)/shard_map/ppermute | solution.py:216
  25.7 22.2 %all_to_all.20.second_ref = bf16[16,48,128]{2,1,0:T(8,128)(2,1)S(1)} all-to-all(bf16[16,48,128]{2,1,0:T(8,128)(2,1)S(1)} %broadcast_in_dim.4), channel_id=1, replica_groups=mesh['yq'=4,'yp'=2,'zq'=4,'zp'=2,'c'=2,'x'=4] {'yq','zq'}, dimensions={0} | all-to-all | bytes 393216 | tf_op jit(solution)/shard_map/all_to_all | solution.py:32
  47.9 1.3 %block.1 = (bf16[32,40,128]{2,1,0:T(8,128)(2,1)}, bf16[16,40,128]{2,1,0:T(8,128)(2,1)S(1)}, f32[8,128]{1,0:T(8,128)S(1)}) custom-call(f32[8,128]{1,0:T(8,128)S(1)} %select_maximum_fusion.row_ref, bf16[32,64,128]{2,1,0:T(8,128)(2,1)S(1)} %all-to-all-done.first_ref, bf16[16,48,128]{2,1,0:T(8,128)(2,1)S(1)} %all_to_all.20.second_ref), custom_call_target="tpu_custom_call" | custom-call | tf_op jit(solution)/shard_map/block/pallas_call | solution.py:146
  49.2 16.7 %all_to_all.21 = bf16[16,40,128]{2,1,0:T(8,128)(2,1)S(1)} all-to-all(bf16[16,40,128]{2,1,0:T(8,128)(2,1)S(1)} %get-tuple-element.27), channel_id=1, replica_groups=mesh['yq'=4,'yp'=2,'zq'=4,'zp'=2,'c'=2,'x'=4] {'yq','zq'}, dimensions={0} | all-to-all | bytes 327680 | tf_op jit(solution)/shard_map/all_to_all | solution.py:32
  66.0 6.7 %all-to-all-start.2 = ((bf16[32,40,128]{2,1,0:T(8,128)(2,1)}), bf16[32,40,128]{2,1,0:T(8,128)(2,1)S(1)}, u32[]{:S(2)}, u32[]{:S(2)}) async-start(bf16[32,40,128]{2,1,0:T(8,128)(2,1)} %get-tuple-element.19), calls=%async_computation.2 | async-start | bytes 655360 | tf_op jit(solution)/shard_map/all_to_all | solution.py:32
  72.7 3.5 %collective-permute-start.1 = (bf16[40,128]{1,0:T(8,128)(2,1)S(1)}, bf16[40,128]{1,0:T(8,128)(2,1)S(1)}, u32[]{:S(2)}, u32[]{:S(2)}) collective-permute-start(bf16[40,128]{1,0:T(8,128)(2,1)S(1)} %reduce_sum.12), channel_id=1, source_target_pairs={{0,0},{1,128},{2,256},{3,384},{128,1},{129,129},{130,257},{131,385... | collective-permute-start | bytes 30728 | tf_op jit(solution)/shard_map/ppermute | solution.py:223
  76.1 0.6 fusion.3
  76.7 0.1 slice.7
  76.8 0.1 broadcast_in_dim.10
  76.9 0.1 reshape.20.row_ref
  77.0 7.5 %collective-permute-done.1 = bf16[40,128]{1,0:T(8,128)(2,1)S(1)} collective-permute-done((bf16[40,128]{1,0:T(8,128)(2,1)S(1)}, bf16[40,128]{1,0:T(8,128)(2,1)S(1)}, u32[]{:S(2)}, u32[]{:S(2)}) %collective-permute-start.1) | collective-permute-done | bytes 10272 | tf_op jit(solution)/shard_map/ppermute | solution.py:223
  84.5 0.0 all-to-all-done.2.grad_ref
  84.5 0.0 copy-done.2
  84.6 2.0 %adam.1 = (f32[32,5120]{1,0:T(8,128)}, f32[32,5120]{1,0:T(8,128)}, f32[32,5120]{1,0:T(8,128)}, bf16[32,5120]{1,0:T(8,128)(2,1)}) custom-call(bf16[32,40,128]{2,1,0:T(8,128)(2,1)S(1)} %all-to-all-done.2.grad_ref, f32[8,5120]{1,0:T(8,128)S(1)} %reshape.20.row_ref, f32[32,5120]{1,0:T(8,128)S(1)} %copy-done, f32[32,5120]{1,0:T(8,128)S(1)} %copy-done.1, ...), custom_call_target="tpu_custom_call" | custom-call | tf_op jit(solution)/shard_map/adam/pallas_call | solution.py:190
  86.5 0.6 copy.16
  (11 shorter events, 0.1 us)
Async XLA Ops:
  4.2 9.5 %copy-start.4 = (bf16[128,40]{0,1:T(8,128)(2,1)S(1)}, bf16[128,40]{0,1:T(8,128)(2,1)}, u32[]{:S(2)}) copy-start(bf16[128,40]{0,1:T(8,128)(2,1)} %param.9) | copy-start | bytes 30724
  4.2 18.6 %all-to-all-start = ((bf16[32,64,128]{2,1,0:T(8,128)(2,1)}), bf16[32,64,128]{2,1,0:T(8,128)(2,1)S(1)}, u32[]{:S(2)}, u32[]{:S(2)}) async-start(bf16[32,64,128]{2,1,0:T(8,128)(2,1)} %pack.1), calls=%async_computation | async-start | bytes 1048576 | tf_op jit(solution)/shard_map/all_to_all | solution.py:32
  13.7 11.9 %collective-permute-start = (bf16[40,128]{1,0:T(8,128)(2,1)S(1)}, bf16[40,128]{1,0:T(8,128)(2,1)S(1)}, u32[]{:S(2)}, u32[]{:S(2)}) collective-permute-start(bf16[40,128]{1,0:T(8,128)(2,1)S(1)} %bitcast.19), channel_id=1, source_target_pairs={{0,0},{1,128},{2,256},{3,384},{128,1},{129,129},{130,257},{131,385... | collective-permute-start | bytes 30728 | tf_op jit(solution)/shard_map/ppermute | solution.py:216
  19.2 0.7 copy-start.3
  47.9 36.7 %copy-start.2 = (f32[32,5120]{1,0:T(8,128)S(1)}, f32[32,5120]{1,0:T(8,128)}, u32[]{:S(2)}) copy-start(f32[32,5120]{1,0:T(8,128)} %two_ref.1) | copy-start | bytes 1966084
  65.9 18.6 %copy-start = (f32[32,5120]{1,0:T(8,128)S(1)}, f32[32,5120]{1,0:T(8,128)}, u32[]{:S(2)}) copy-start(f32[32,5120]{1,0:T(8,128)} %master_ref.1) | copy-start | bytes 1966084
  66.0 18.6 %copy-start.1 = (f32[32,5120]{1,0:T(8,128)S(1)}, f32[32,5120]{1,0:T(8,128)}, u32[]{:S(2)}) copy-start(f32[32,5120]{1,0:T(8,128)} %one_ref.1) | copy-start | bytes 1966084
  66.0 18.6 %all-to-all-start.2 = ((bf16[32,40,128]{2,1,0:T(8,128)(2,1)}), bf16[32,40,128]{2,1,0:T(8,128)(2,1)S(1)}, u32[]{:S(2)}, u32[]{:S(2)}) async-start(bf16[32,40,128]{2,1,0:T(8,128)(2,1)} %get-tuple-element.19), calls=%async_computation.2 | async-start | bytes 655360 | tf_op jit(solution)/shard_map/all_to_all | solution.py:32
  72.7 11.9 %collective-permute-start.1 = (bf16[40,128]{1,0:T(8,128)(2,1)S(1)}, bf16[40,128]{1,0:T(8,128)(2,1)S(1)}, u32[]{:S(2)}, u32[]{:S(2)}) collective-permute-start(bf16[40,128]{1,0:T(8,128)(2,1)S(1)} %reduce_sum.12), channel_id=1, source_target_pairs={{0,0},{1,128},{2,256},{3,384},{128,1},{129,129},{130,257},{131,385... | collective-permute-start | bytes 30728 | tf_op jit(solution)/shard_map/ppermute | solution.py:223

commit v8 on v7

--- a/solution.py
+++ b/solution.py
@@ -9,7 +9,7 @@
 BUCKETS = 16
 FSDP = ("yq", "yp", "zq", "zp", "c")
 ALL = FSDP + ("x",)
-NEAR = ("x", "yp", "zp", "c")
+NEAR = ("yp", "zp", "c", "x")
 FAR = ("yq", "zq")
 NX, NE, NFAR = 4, 8, 16
 STEPS = 2
@@ -38,7 +38,8 @@
         pltpu.make_async_copy(tok_hbm, tok_ref, sems.at[0]),
         pltpu.make_async_copy(flag_hbm, flag_ref, sems.at[1]),
         *[
-            pltpu.make_async_copy(ref.at[mine], parts_ref.at[k], sems.at[2 + k])
+            pltpu.make_async_copy(ref.at[mine, pl.ds(x * 1280, 1280)], parts_ref.at[x, k], sems.at[2 + 3 * x + k])
+            for x in range(NX)
             for k, ref in enumerate((master_hbm, one_hbm, two_hbm))
         ],
     ]
@@ -47,32 +48,32 @@
     reads[0].wait()
     reads[1].wait()
     tok = tok_ref[...]
-    for d in range(NX * NE):
-        out_ref[d, 0:32, :] = tok
+    for x in range(NX):
+        for e in range(NE):
+            out_ref[e, x, 0:32, :] = tok
     flag = jnp.concatenate([flag_ref[...].astype(f32), jnp.zeros((1, 32 - BUCKETS), f32)], axis=1)
     flag = jnp.broadcast_to(flag, (8, 32))
-    for read in reads[2:]:
-        read.wait()
     writes = []
     for x in range(NX):
+        for read in reads[2 + 3 * x : 5 + 3 * x]:
+            read.wait()
         for e in range(NE):
-            d = x * NE + e
+            first = [c - 1280 * x for c in runs(x, e)]
             parts = [
-                jnp.concatenate([parts_ref[k, :, c : c + 40] for c in runs(x, e)], axis=1) for k in range(3)
+                jnp.concatenate([parts_ref[x, k, :, c : c + 40] for c in first], axis=1) for k in range(3)
             ]
             main = [p[:, :LANES] for p in parts]
             rest = jnp.concatenate([p[:, LANES:] for p in parts] + [flag], axis=1)
-            out_ref[d, 32:48, :] = jnp.concatenate(main[:2], axis=0).astype(bf16)
-            out_ref[d, 48:64, :] = jnp.concatenate([main[2], rest], axis=0).astype(bf16)
-        here = pl.ds(x * NE, NE)
-        writes.append(pltpu.make_async_copy(out_ref.at[here], out_hbm.at[here], sent.at[x]))
+            out_ref[e, x, 32:48, :] = jnp.concatenate(main[:2], axis=0).astype(bf16)
+            out_ref[e, x, 48:64, :] = jnp.concatenate([main[2], rest], axis=0).astype(bf16)
+        writes.append(pltpu.make_async_copy(out_ref.at[:, x], out_hbm.at[:, x], sent.at[x]))
         writes[-1].start()
     for write in writes:
         write.wait()
 
 
 def pack(tok, flag, master, one, two):
-    out = (NX * NE, 64, LANES)
+    out = (NE, NX, 64, LANES)
     anywhere = pl.BlockSpec(memory_space=pl.ANY)
     return pl.pallas_call(
         pack_kernel,
@@ -82,13 +83,13 @@
         scratch_shapes=[
             pltpu.VMEM(tok.shape, bf16),
             pltpu.VMEM(flag.shape, jnp.int32),
-            pltpu.VMEM((3, 8, master.shape[1]), f32),
+            pltpu.VMEM((NX, 3, 8, master.shape[1] // NX), f32),
             pltpu.VMEM(out, bf16),
-            pltpu.SemaphoreType.DMA((5,)),
+            pltpu.SemaphoreType.DMA((2 + 3 * NX,)),
             pltpu.SemaphoreType.DMA((NX,)),
         ],
         name="pack",
-    )(tok, flag, master, one, two)
+    )(tok, flag, master, one, two).reshape(NE * NX, 64, LANES)
 
 
 def update(master, one, two, gradient, scale, fix):
@@ -98,7 +99,7 @@
 
 
 def block_kernel(row_ref, first_ref, second_ref, grad_hbm, part_ref, count_ref, message, sent):
-    tok = [first_ref[x * NE : (x + 1) * NE, 0:32, :].reshape(NE * 32, LANES) for x in range(NX)]
+    tok = [jnp.concatenate([first_ref[e * NX + x, 0:32, :] for e in range(NE)], axis=0) for x in range(NX)]
     tok = jnp.concatenate(tok, axis=1)
     og = [second_ref[x * NX : (x + 1) * NX, 0:40, :].reshape(160, LANES) for x in range(NX)]
     og = jnp.concatenate(og, axis=1)
@@ -107,7 +108,7 @@
         g = grad[y * 32 : (y + 1) * 32, :]
         tail = jnp.concatenate([g[8 * k : 8 * k + 8, LANES:160] for k in range(4)], axis=1)
         message[y] = jnp.concatenate([g[:, :LANES], tail], axis=0).astype(bf16)
-    writes = [pltpu.make_async_copy(message, grad_hbm.at[pl.ds(x * NE, NE)], sent.at[x]) for x in range(NX)]
+    writes = [pltpu.make_async_copy(message, grad_hbm.at[:, x], sent.at[x]) for x in range(NX)]
     for write in writes:
         write.start()
     count = jnp.max(second_ref[:, 40:48, :].astype(f32), axis=0)
@@ -117,7 +118,7 @@
     table = [count, *[jnp.broadcast_to(row_ref[k : k + 1, :], (8, LANES)) for k in range(2)]]
     pick = lambda v, b: jnp.max(jnp.where(lane == b, v, 0.0), axis=(0, 1), keepdims=True)
     both = [[pick(v, bucket + k) for k in range(2)] for v in table]
-    order = [x * NE + y for y in range(NE) for x in range(NX)]
+    order = range(NE * NX)
     pairs = [[first_ref[d, 32 + 16 * k : 48 + 16 * k, :].astype(f32) for d in order] for k in range(2)]
     params = [
         jnp.concatenate([p[8 * half : 8 * half + 8] for p in pairs[k]], axis=0) for k in range(2) for half in range(2)
@@ -146,7 +147,7 @@
     return pl.pallas_call(
         block_kernel,
         out_shape=(
-            jax.ShapeDtypeStruct((NX * NE, 40, LANES), bf16),
+            jax.ShapeDtypeStruct((NE, NX, 40, LANES), bf16),
             jax.ShapeDtypeStruct((NFAR, 40, LANES), bf16),
             jax.ShapeDtypeStruct((8, LANES), f32),
         ),
@@ -164,10 +165,10 @@
     here = pl.ds(pl.multiple_of(i * step, LANES), step)
     pieces = []
     for y in range(NE // STEPS):
-        block = i * (NE // STEPS) + y
+        x, yp = i * (NE // STEPS // 2) + y // 2, y % 2
         got = []
         for zc in range(4):
-            g = grad_ref[block * 4 + zc].astype(f32)
+            g = grad_ref[(yp * 4 + zc) * NX + x].astype(f32)
             tail = g[32:40]
             tail = jnp.concatenate([tail[:, 32 * k : 32 * k + 32] for k in range(4)], axis=0)
             got.append(jnp.concatenate([g[:32], tail], axis=1))
@@ -221,7 +222,7 @@
     grad, part, count = block(own, first, second)
     total = jnp.sum(exchange(part, FAR).astype(f32), axis=0)
     result = lax.ppermute(total.astype(bf16), ("yq", "x"), perm)
-    grad = exchange(grad, NEAR)
+    grad = exchange(grad.reshape(NE * NX, 40, LANES), NEAR)
 
     counts = count[0, FLAGS : FLAGS + BUCKETS]
     row = jnp.stack([counts, scales, fixes, *[counts] * 5])

time: 87.7 us -> 86.3 us (0.984)
  Pallas kernels: 6.87 us -> 5.74 us
    pallas_call x1, Pallas kernels: 3.56 us -> 2.42 us  [pack(): pl.pallas_call(pack_kernel, out_shape=jax.ShapeDtypeStruct(out, bf16), in...]
where the time goes in v8:
time: 86.3 us; the launch traced here: 85.8 us
  blocking collectives  38.9 us (45%)
  starting transfers between devices  24.6 us (29%)
  waiting for transfers between devices  12.9 us (15%)
  Pallas kernels  5.74 us (7%)
  local copies, waits for them, and re-layouts  1.59 us (2%)
  between operations  1.39 us (2%)
    all_to_all x2, blocking collectives, exchange(): return lax.all_to_all(x, axes, 0, 0, tiled=True)  38.9 us
    all_to_all x2, starting transfers between devices, exchange(): return lax.all_to_all(x, axes, 0, 0, tiled=True)  16.1 us
    ppermute x1, waiting for transfers between devices, local(): result = lax.ppermute(total.astype(bf16), ('yq', 'x'), perm)  7.34 us
    ppermute x1, starting transfers between devices, local(): og = lax.ppermute(out_grad.T, ('yq', 'x'), perm)  4.89 us
    ppermute x1, starting transfers between devices, local(): result = lax.ppermute(total.astype(bf16), ('yq', 'x'), perm)  3.65 us
    ppermute x1, waiting for transfers between devices, local(): og = lax.ppermute(out_grad.T, ('yq', 'x'), perm)  2.86 us
    all_to_all x2, waiting for transfers between devices, exchange(): return lax.all_to_all(x, axes, 0, 0, tiled=True)  2.69 us
    pallas_call x1, Pallas kernels, pack(): pl.pallas_call(pack_kernel, out_shape=jax.ShapeDtypeStruct(out, bf16), in...  2.42 us
  transfers between devices with their start and end apart: 4, of which 3 were waited for; matrix products, arithmetic and copies ran while one was open for 1% of the time, Pallas kernels for 0%

profile of v8, /device:TPU:4, one launch (start us, length us, event | category | flops | bytes accessed | tf_op | source)
XLA Modules:
  0.0 85.8 jit_solution(13217695417467540087)
XLA Ops:
  0.6 2.4 %pack.1 = bf16[8,4,64,128]{3,2,1,0:T(8,128)(2,1)} custom-call(bf16[32,128]{1,0:T(8,128)(2,1)} %bitcast.17, s32[1,16]{1,0:T(1,128)} %flag_hbm.1, f32[32,5120]{1,0:T(8,128)} %master_ref.1, f32[32,5120]{1,0:T(8,128)} %one_ref.1, f32[32,5120]{1,0:T(8,128)} %two_ref.1), custom_call_target="tpu_custom_call" | custom-call | tf_op jit(solution)/shard_map/pack/pallas_call | solution.py:78
  3.1 0.0 copy-start.4
  3.1 9.4 %all-to-all-start = ((bf16[32,64,128]{2,1,0:T(8,128)(2,1)}), bf16[32,64,128]{2,1,0:T(8,128)(2,1)S(1)}, u32[]{:S(2)}, u32[]{:S(2)}) async-start(bf16[32,64,128]{2,1,0:T(8,128)(2,1)} %bitcast.15), calls=%async_computation | async-start | bytes 1048576 | tf_op jit(solution)/shard_map/all_to_all | solution.py:32
  12.5 0.0 copy-done.4
  12.5 4.9 %collective-permute-start = (bf16[40,128]{1,0:T(8,128)(2,1)S(1)}, bf16[40,128]{1,0:T(8,128)(2,1)S(1)}, u32[]{:S(2)}, u32[]{:S(2)}) collective-permute-start(bf16[40,128]{1,0:T(8,128)(2,1)S(1)} %bitcast.22), channel_id=1, source_target_pairs={{0,0},{1,128},{2,256},{3,384},{128,1},{129,129},{130,257},{131,385... | collective-permute-start | bytes 30728 | tf_op jit(solution)/shard_map/ppermute | solution.py:217
  18.0 0.0 copy-start.3
  18.1 0.6 copy-done.3
  18.7 0.1 select_maximum_fusion.row_ref
  18.8 2.7 %all-to-all-done.first_ref = bf16[32,64,128]{2,1,0:T(8,128)(2,1)S(1)} async-done(((bf16[32,64,128]{2,1,0:T(8,128)(2,1)}), bf16[32,64,128]{2,1,0:T(8,128)(2,1)S(1)}, u32[]{:S(2)}, u32[]{:S(2)}) %all-to-all-start) | async-done | bytes 524320 | tf_op jit(solution)/shard_map/all_to_all | solution.py:32
  21.5 2.9 %collective-permute-done = bf16[40,128]{1,0:T(8,128)(2,1)S(1)} collective-permute-done((bf16[40,128]{1,0:T(8,128)(2,1)S(1)}, bf16[40,128]{1,0:T(8,128)(2,1)S(1)}, u32[]{:S(2)}, u32[]{:S(2)}) %collective-permute-start) | collective-permute-done | bytes 10272 | tf_op jit(solution)/shard_map/ppermute | solution.py:217
  24.4 22.1 %all_to_all.20.second_ref = bf16[16,48,128]{2,1,0:T(8,128)(2,1)S(1)} all-to-all(bf16[16,48,128]{2,1,0:T(8,128)(2,1)S(1)} %broadcast_in_dim.4), channel_id=1, replica_groups=mesh['yq'=4,'yp'=2,'zq'=4,'zp'=2,'c'=2,'x'=4] {'yq','zq'}, dimensions={0} | all-to-all | bytes 393216 | tf_op jit(solution)/shard_map/all_to_all | solution.py:32
  46.5 1.3 %block.1 = (bf16[8,4,40,128]{3,2,1,0:T(8,128)(2,1)}, bf16[16,40,128]{2,1,0:T(8,128)(2,1)S(1)}, f32[8,128]{1,0:T(8,128)S(1)}) custom-call(f32[8,128]{1,0:T(8,128)S(1)} %select_maximum_fusion.row_ref, bf16[32,64,128]{2,1,0:T(8,128)(2,1)S(1)} %all-to-all-done.first_ref, bf16[16,48,128]{2,1,0:T(8,128)(2,1)S(1)} %all_to_all.20.second_ref), custom_call_target="tpu_custom_call" | custom-call | tf_op jit(solution)/shard_map/block/pallas_call | solution.py:147
  47.9 16.7 %all_to_all.21 = bf16[16,40,128]{2,1,0:T(8,128)(2,1)S(1)} all-to-all(bf16[16,40,128]{2,1,0:T(8,128)(2,1)S(1)} %get-tuple-element.27), channel_id=1, replica_groups=mesh['yq'=4,'yp'=2,'zq'=4,'zp'=2,'c'=2,'x'=4] {'yq','zq'}, dimensions={0} | all-to-all | bytes 327680 | tf_op jit(solution)/shard_map/all_to_all | solution.py:32
  64.6 6.7 %all-to-all-start.2 = ((bf16[32,40,128]{2,1,0:T(8,128)(2,1)}), bf16[32,40,128]{2,1,0:T(8,128)(2,1)S(1)}, u32[]{:S(2)}, u32[]{:S(2)}) async-start(bf16[32,40,128]{2,1,0:T(8,128)(2,1)} %bitcast.6), calls=%async_computation.2 | async-start | bytes 655360 | tf_op jit(solution)/shard_map/all_to_all | solution.py:32
  71.3 3.6 %collective-permute-start.1 = (bf16[40,128]{1,0:T(8,128)(2,1)S(1)}, bf16[40,128]{1,0:T(8,128)(2,1)S(1)}, u32[]{:S(2)}, u32[]{:S(2)}) collective-permute-start(bf16[40,128]{1,0:T(8,128)(2,1)S(1)} %reduce_sum.12), channel_id=1, source_target_pairs={{0,0},{1,128},{2,256},{3,384},{128,1},{129,129},{130,257},{131,385... | collective-permute-start | bytes 30728 | tf_op jit(solution)/shard_map/ppermute | solution.py:224
  75.0 0.6 fusion.3
  75.6 0.1 slice.7
  75.7 0.1 broadcast_in_dim.10
  75.8 0.1 reshape.28.row_ref
  75.9 7.3 %collective-permute-done.1 = bf16[40,128]{1,0:T(8,128)(2,1)S(1)} collective-permute-done((bf16[40,128]{1,0:T(8,128)(2,1)S(1)}, bf16[40,128]{1,0:T(8,128)(2,1)S(1)}, u32[]{:S(2)}, u32[]{:S(2)}) %collective-permute-start.1) | collective-permute-done | bytes 10272 | tf_op jit(solution)/shard_map/ppermute | solution.py:224
  83.2 0.0 all-to-all-done.2.grad_ref
  83.2 0.0 copy-done.2
  83.2 2.0 %adam.1 = (f32[32,5120]{1,0:T(8,128)}, f32[32,5120]{1,0:T(8,128)}, f32[32,5120]{1,0:T(8,128)}, bf16[32,5120]{1,0:T(8,128)(2,1)}) custom-call(bf16[32,40,128]{2,1,0:T(8,128)(2,1)S(1)} %all-to-all-done.2.grad_ref, f32[8,5120]{1,0:T(8,128)S(1)} %reshape.28.row_ref, f32[32,5120]{1,0:T(8,128)S(1)} %copy-done, f32[32,5120]{1,0:T(8,128)S(1)} %copy-done.1, ...), custom_call_target="tpu_custom_call" | custom-call | tf_op jit(solution)/shard_map/adam/pallas_call | solution.py:191
  85.2 0.6 copy.16
  (11 shorter events, 0.1 us)
Async XLA Ops:
  3.1 9.4 %copy-start.4 = (bf16[128,40]{0,1:T(8,128)(2,1)S(1)}, bf16[128,40]{0,1:T(8,128)(2,1)}, u32[]{:S(2)}) copy-start(bf16[128,40]{0,1:T(8,128)(2,1)} %param.9) | copy-start | bytes 30724
  3.1 18.4 %all-to-all-start = ((bf16[32,64,128]{2,1,0:T(8,128)(2,1)}), bf16[32,64,128]{2,1,0:T(8,128)(2,1)S(1)}, u32[]{:S(2)}, u32[]{:S(2)}) async-start(bf16[32,64,128]{2,1,0:T(8,128)(2,1)} %bitcast.15), calls=%async_computation | async-start | bytes 1048576 | tf_op jit(solution)/shard_map/all_to_all | solution.py:32
  12.5 11.9 %collective-permute-start = (bf16[40,128]{1,0:T(8,128)(2,1)S(1)}, bf16[40,128]{1,0:T(8,128)(2,1)S(1)}, u32[]{:S(2)}, u32[]{:S(2)}) collective-permute-start(bf16[40,128]{1,0:T(8,128)(2,1)S(1)} %bitcast.22), channel_id=1, source_target_pairs={{0,0},{1,128},{2,256},{3,384},{128,1},{129,129},{130,257},{131,385... | collective-permute-start | bytes 30728 | tf_op jit(solution)/shard_map/ppermute | solution.py:217
  18.0 0.7 copy-start.3
  46.5 36.7 %copy-start.2 = (f32[32,5120]{1,0:T(8,128)S(1)}, f32[32,5120]{1,0:T(8,128)}, u32[]{:S(2)}) copy-start(f32[32,5120]{1,0:T(8,128)} %two_ref.1) | copy-start | bytes 1966084
  64.6 18.6 %copy-start = (f32[32,5120]{1,0:T(8,128)S(1)}, f32[32,5120]{1,0:T(8,128)}, u32[]{:S(2)}) copy-start(f32[32,5120]{1,0:T(8,128)} %master_ref.1) | copy-start | bytes 1966084
  64.6 18.6 %copy-start.1 = (f32[32,5120]{1,0:T(8,128)S(1)}, f32[32,5120]{1,0:T(8,128)}, u32[]{:S(2)}) copy-start(f32[32,5120]{1,0:T(8,128)} %one_ref.1) | copy-start | bytes 1966084
  64.6 18.6 %all-to-all-start.2 = ((bf16[32,40,128]{2,1,0:T(8,128)(2,1)}), bf16[32,40,128]{2,1,0:T(8,128)(2,1)S(1)}, u32[]{:S(2)}, u32[]{:S(2)}) async-start(bf16[32,40,128]{2,1,0:T(8,128)(2,1)} %bitcast.6), calls=%async_computation.2 | async-start | bytes 655360 | tf_op jit(solution)/shard_map/all_to_all | solution.py:32
  71.3 11.9 %collective-permute-start.1 = (bf16[40,128]{1,0:T(8,128)(2,1)S(1)}, bf16[40,128]{1,0:T(8,128)(2,1)S(1)}, u32[]{:S(2)}, u32[]{:S(2)}) collective-permute-start(bf16[40,128]{1,0:T(8,128)(2,1)S(1)} %reduce_sum.12), channel_id=1, source_target_pairs={{0,0},{1,128},{2,256},{3,384},{128,1},{129,129},{130,257},{131,385... | collective-permute-start | bytes 30728 | tf_op jit(solution)/shard_map/ppermute | solution.py:224
